TPU v7x, 32 devices: a whole 2x2x4 slice. The times are simulated.
32 devices in a mesh: rep: 16 (over z, x, core), tp: 2 (over y).
Axes of the slice: x: 2, y: 2, z: 4, core: 2. Of those that a mesh axis runs over, the one named last changes fastest.
Arguments:
- tokens: bfloat16 [16, 256, 3072], P('rep', 'tp'), may hold values from -100 to 100
- norm_gain: float32 [16, 3072], P('rep'), may hold values from 0.5 to 1.5
- w_query: bfloat16 [16, 3072, 2048], P('rep', None, 'tp'), may hold values from -1 to 1
- key_weight: bfloat16 [16, 3072, 1024], P('rep', None, 'tp'), may hold values from -1 to 1
- value_weight: bfloat16 [16, 3072, 1024], P('rep', None, 'tp'), may hold values from -0.109375 to 0.109375
- attention_gradient: bfloat16 [16, 256, 2048], P('rep', None, 'tp'), may hold values from -6 to 6
- global_fragment: float32 [128, 3072], P('tp'), may hold values from -6 to 6
- momentum: float32 [128, 3072], P('tp'), may hold values from -3 to 3
- local_fragment: bfloat16 [16, 128, 3072], P('rep', 'tp'), may hold values from -6 to 6
Outputs:
- grad_query_w: bfloat16 [16, 3072, 2048], P('rep', None, 'tp')
- grad_key_w: bfloat16 [16, 3072, 1024], P('rep', None, 'tp')
- grad_value_w: bfloat16 [16, 3072, 1024], P('rep', None, 'tp')
- grad_gain: float32 [16, 3072], P('rep')
- grad_tokens: bfloat16 [16, 256, 3072], P('rep', 'tp')
- new_global: float32 [128, 3072], P('tp')
- new_momentum: float32 [128, 3072], P('tp')
All inputs are finite; a program needn't handle non-finite values.
Results may differ from a plain program's by a relative error of at most 0.019.
The roundings to bfloat16 on the way count: a program that leaves them out, or rounds other values in their place, can miss the bound.
Values may be sent and summed in bfloat16 or wider, within the bound.
A program may use at most 128 MiB of HBM per device.

v0:
```python
import functools

import jax
import jax.numpy as jnp
import numpy as np
from jax import lax
from jax.experimental import pallas as pl
from jax.experimental.pallas import tpu as pltpu
from jax.sharding import PartitionSpec as P

MESH = pl.DeviceIdType.MESH

HEAD_SIZE = 128


epsilon = 1e-05
rope_base = 500000.0
outer_rate = 0.7
outer_momentum = 0.9


def rope_tables(sequence_length, width):
    middle = width // 2
    frequency = rope_base ** (-2.0 * jnp.arange(middle, dtype=jnp.float32) / width)
    angles = jnp.arange(sequence_length, dtype=jnp.float32)[:, None] * frequency[None, :]
    angles = jnp.concatenate([angles, angles], axis=1)
    return (jnp.cos(angles)[:, None, :], jnp.sin(angles)[:, None, :])


def rotate(vectors, cosine_table, sine_table):
    middle = vectors.shape[-1] // 2
    turned = jnp.concatenate([-vectors[..., middle:], vectors[..., :middle]], axis=-1)
    return vectors * cosine_table + turned * sine_table


def reverse_rotation(gradient, cosine_table, sine_table):
    middle = gradient.shape[-1] // 2
    shifted = gradient * sine_table
    turned = jnp.concatenate([shifted[..., middle:], -shifted[..., :middle]], axis=-1)
    return gradient * cosine_table + turned


def attention_reverse(query_rows, rotated_keys, values_bfloat, grad_out, block_of_rows):
    sequence_length = query_rows.shape[0]
    score_scale = query_rows.shape[-1] ** (-0.5)

    def one_block(running, block_index):
        acc_key, acc_value = running
        offset = block_index * block_of_rows
        query_block = lax.dynamic_slice_in_dim(query_rows, offset, block_of_rows, 0)
        grad_block = lax.dynamic_slice_in_dim(grad_out, offset, block_of_rows, 0)
        scores = (
            jnp.einsum(
                "qgrd,kgd->grqk", query_block, rotated_keys, preferred_element_type=jnp.float32
            )
            * score_scale
        )
        row_pos = offset + jnp.arange(block_of_rows)
        col_pos = jnp.arange(sequence_length)
        allowed = col_pos[None, :] <= row_pos[:, None]
        scores = jnp.where(allowed, scores, -jnp.inf)
        highest = jnp.max(scores, axis=-1, keepdims=True)
        powers = jnp.exp(scores - highest)
        probability = powers / jnp.sum(powers, axis=-1, keepdims=True)
        prob_low = probability.astype(jnp.bfloat16)
        acc_value = acc_value + jnp.einsum(
            "grqk,qgrd->kgd", prob_low, grad_block, preferred_element_type=jnp.float32
        )
        grad_prob = jnp.einsum(
            "qgrd,kgd->grqk", grad_block, values_bfloat, preferred_element_type=jnp.float32
        )
        grad_score = (
            probability
            * (grad_prob - jnp.sum(grad_prob * probability, axis=-1, keepdims=True))
            * score_scale
        )
        score_low = grad_score.astype(jnp.bfloat16)
        grad_query = jnp.einsum(
            "grqk,kgd->qgrd", score_low, rotated_keys, preferred_element_type=jnp.float32
        )
        acc_key = acc_key + jnp.einsum(
            "grqk,qgrd->kgd", score_low, query_block, preferred_element_type=jnp.float32
        )
        return ((acc_key, acc_value), grad_query)

    initial = jnp.zeros(rotated_keys.shape, jnp.float32)
    (acc_key, acc_value), grad_blocks = lax.scan(
        one_block, (initial, initial), jnp.arange(sequence_length // block_of_rows)
    )
    return (grad_blocks.reshape(query_rows.shape), acc_key, acc_value)


def body(
    tokens,
    norm_gain,
    w_query,
    key_weight,
    value_weight,
    attention_gradient,
    global_fragment,
    momentum,
    local_fragment,
):
    local_rows = tokens[0]
    norm_gains = norm_gain[0]
    weight_q = w_query[0]
    weight_k = key_weight[0]
    weight_v = value_weight[0]
    widened_rows = local_rows.astype(jnp.float32)
    inverse_norm = lax.rsqrt(
        jnp.mean(widened_rows * widened_rows, axis=-1, keepdims=True) + epsilon
    )
    normalized_input = widened_rows * inverse_norm
    normalized_local = (normalized_input * norm_gains[None, :]).astype(jnp.bfloat16)
    normalized = lax.all_gather(normalized_local, "tp", axis=0, tiled=True)
    sequence_length = normalized.shape[0]
    heads_q = weight_q.shape[1] // HEAD_SIZE
    heads_kv = weight_k.shape[1] // HEAD_SIZE
    cosine_table, sine_table = rope_tables(sequence_length, HEAD_SIZE)
    query_rows = jnp.dot(normalized, weight_q, preferred_element_type=jnp.float32).reshape(
        sequence_length, heads_q, HEAD_SIZE
    )
    query_rows = rotate(query_rows, cosine_table, sine_table).astype(jnp.bfloat16)
    rotated_keys = jnp.dot(normalized, weight_k, preferred_element_type=jnp.float32).reshape(
        sequence_length, heads_kv, HEAD_SIZE
    )
    rotated_keys = rotate(rotated_keys, cosine_table, sine_table).astype(jnp.bfloat16)
    values_bfloat = (
        jnp.dot(normalized, weight_v, preferred_element_type=jnp.float32)
        .astype(jnp.bfloat16)
        .reshape(sequence_length, heads_kv, HEAD_SIZE)
    )
    replica_group = heads_q // heads_kv
    block_of_rows = min(512, sequence_length)
    query_input_gradient, key_input_gradient, value_input_gradient = attention_reverse(
        query_rows.reshape(sequence_length, heads_kv, replica_group, HEAD_SIZE),
        rotated_keys,
        values_bfloat,
        attention_gradient[0].reshape(sequence_length, heads_kv, replica_group, HEAD_SIZE),
        block_of_rows,
    )
    dquery = (
        reverse_rotation(
            query_input_gradient.reshape(sequence_length, heads_q, HEAD_SIZE),
            cosine_table,
            sine_table,
        )
        .astype(jnp.bfloat16)
        .reshape(sequence_length, heads_q * HEAD_SIZE)
    )
    key_gradient = (
        reverse_rotation(key_input_gradient, cosine_table, sine_table)
        .astype(jnp.bfloat16)
        .reshape(sequence_length, heads_kv * HEAD_SIZE)
    )
    value_gradient = value_input_gradient.astype(jnp.bfloat16).reshape(
        sequence_length, heads_kv * HEAD_SIZE
    )
    contract = (((0,), (0,)), ((), ()))
    grad_wq = lax.dot_general(
        normalized, dquery, contract, preferred_element_type=jnp.float32
    ).astype(jnp.bfloat16)
    grad_wk = lax.dot_general(
        normalized, key_gradient, contract, preferred_element_type=jnp.float32
    ).astype(jnp.bfloat16)
    grad_wv = lax.dot_general(
        normalized, value_gradient, contract, preferred_element_type=jnp.float32
    ).astype(jnp.bfloat16)
    back = (((1,), (1,)), ((), ()))
    partial_value = lax.dot_general(dquery, weight_q, back, preferred_element_type=jnp.float32)
    partial_value = partial_value + lax.dot_general(
        key_gradient, weight_k, back, preferred_element_type=jnp.float32
    )
    summed_rows = lax.psum_scatter(
        (
            partial_value
            + lax.dot_general(value_gradient, weight_v, back, preferred_element_type=jnp.float32)
        ).astype(jnp.bfloat16),
        "tp",
        scatter_dimension=0,
        tiled=True,
    ).astype(jnp.float32)
    gains_gradient = lax.psum(jnp.sum(summed_rows * normalized_input, axis=0), "tp")
    scaled_rows = summed_rows * norm_gains[None, :]
    gradient_rows = (
        inverse_norm
        * (
            scaled_rows
            - normalized_input * jnp.mean(scaled_rows * normalized_input, axis=-1, keepdims=True)
        )
    ).astype(jnp.bfloat16)
    delta = global_fragment - local_fragment[0].astype(jnp.float32)
    replicas = lax.axis_size("rep")
    mean_delta = lax.psum(delta, "rep") / replicas
    new_momentum = outer_momentum * momentum + mean_delta
    new_global = global_fragment - outer_rate * (mean_delta + outer_momentum * new_momentum)
    return (
        grad_wq[None],
        grad_wk[None],
        grad_wv[None],
        gains_gradient[None],
        gradient_rows[None],
        new_global,
        new_momentum,
    )

NT = (((1,), (1,)), ((), ()))
TN = (((0,), (0,)), ((), ()))


def dot(a, b, dims=(((1,), (0,)), ((), ()))):
    return lax.dot_general(a, b, dims, preferred_element_type=jnp.float32)


def ds(index, size):
    return pl.ds(pl.multiple_of(index * size, size), size)


def host_tables(sequence_length, width):
    middle = width // 2
    frequency = rope_base ** (-2.0 * np.arange(middle) / width)
    angles = np.arange(sequence_length)[:, None] * frequency[None, :]
    cosine, sine = np.cos(angles), np.sin(angles)
    return (
        jnp.asarray(np.concatenate([cosine, cosine], axis=1), jnp.float32),
        jnp.asarray(np.concatenate([-sine, sine], axis=1), jnp.float32),
    )


def front_kernel(
    n_rep,
    chunks,
    tile,
    tokens_ref,
    gain_ref,
    wq_hbm,
    wk_hbm,
    wv_hbm,
    go_ref,
    cos_ref,
    sin_ref,
    local_hbm,
    normed_ref,
    dq_ref,
    dk_ref,
    dv_ref,
    mean_ref,
    w_ref,
    nm_ref,
    acc_ref,
    q_ref,
    k_ref,
    v_ref,
    pieces_ref,
    own_mean_ref,
    all_mean_ref,
    w_sems,
    ag_send,
    ag_recv,
    fr_send,
    fr_recv,
    fg_send,
    fg_recv,
    own_sem,
):
    me = lax.axis_index("tp")
    peer = 1 - me
    rep = lax.axis_index("rep")
    rows, width = tokens_ref.shape
    qw, kw = wq_hbm.shape[1], wk_hbm.shape[1]
    total = qw + 2 * kw
    cw = width // chunks
    piece_rows, piece_cols = own_mean_ref.shape
    col_blocks = width // piece_cols
    barrier = pltpu.get_barrier_semaphore()
    pl.semaphore_signal(barrier, inc=1, device_id={"tp": peer}, device_id_type=MESH)

    def greet(j, _):
        pl.semaphore_signal(
            barrier, inc=1, device_id={"rep": lax.rem(rep + j, n_rep)}, device_id_type=MESH
        )
        return 0

    lax.fori_loop(1, n_rep, greet, 0)
    weight_copies = [
        pltpu.make_async_copy(wq_hbm, w_ref.at[:, pl.ds(0, qw)], w_sems.at[0]),
        pltpu.make_async_copy(wk_hbm, w_ref.at[:, pl.ds(qw, kw)], w_sems.at[1]),
        pltpu.make_async_copy(wv_hbm, w_ref.at[:, pl.ds(qw + kw, kw)], w_sems.at[2]),
    ]
    for copy in weight_copies:
        copy.start()

    def piece(owner):
        return (
            ds(owner // col_blocks, piece_rows),
            ds(lax.rem(owner, col_blocks), piece_cols),
        )

    own_piece = pltpu.make_async_copy(local_hbm.at[piece(rep)], pieces_ref.at[0], own_sem)
    own_piece.start()

    step = 16

    def norm_rows(i, _):
        x = tokens_ref[ds(i, step), :].astype(jnp.float32)
        inverse = lax.rsqrt(jnp.mean(x * x, axis=-1, keepdims=True) + epsilon)
        nm_ref[pl.ds(pl.multiple_of(me * rows + i * step, step), step), :] = (
            x * inverse * gain_ref[...]
        ).astype(jnp.bfloat16)
        return 0

    lax.fori_loop(0, rows // step, norm_rows, 0)
    pl.semaphore_wait(barrier, n_rep)

    def gather_copy(c):
        part = nm_ref.at[ds(me, rows), ds(c, cw)]
        return pltpu.make_async_remote_copy(
            src_ref=part,
            dst_ref=part,
            send_sem=ag_send.at[c],
            recv_sem=ag_recv.at[c],
            device_id={"tp": peer},
            device_id_type=MESH,
        )

    def scatter_copy(j):
        target = lax.rem(rep + j, n_rep)
        return pltpu.make_async_remote_copy(
            src_ref=local_hbm.at[piece(target)],
            dst_ref=pieces_ref.at[j],
            send_sem=fr_send.at[j],
            recv_sem=fr_recv.at[j],
            device_id={"rep": target},
            device_id_type=MESH,
        )

    def spread_copy(j, owner):
        return pltpu.make_async_remote_copy(
            src_ref=own_mean_ref,
            dst_ref=all_mean_ref.at[piece(owner)],
            send_sem=fg_send.at[j],
            recv_sem=fg_recv.at[j],
            device_id={"rep": lax.rem(rep + j, n_rep)},
            device_id_type=MESH,
        )

    def start_all(make, low, high):
        def one(j, _):
            make(j).start()
            return 0

        lax.fori_loop(low, high, one, 0)

    def wait_recv_all(make, low, high):
        def one(j, _):
            make(j).wait_recv()
            return 0

        lax.fori_loop(low, high, one, 0)

    def wait_send_all(make, low, high):
        def one(j, _):
            make(j).wait_send()
            return 0

        lax.fori_loop(low, high, one, 0)

    start_all(gather_copy, 0, chunks)
    start_all(scatter_copy, 1, n_rep)

    for copy in weight_copies:
        copy.wait()

    def own_tile(t, _):
        acc_ref[ds(me, rows), ds(t, tile)] = dot(nm_ref[ds(me, rows), :], w_ref[:, ds(t, tile)])
        return 0

    lax.fori_loop(0, total // tile, own_tile, 0)
    acc_ref[ds(peer, rows), :] = jnp.zeros((rows, total), jnp.float32)

    own_piece.wait()
    wait_recv_all(scatter_copy, 1, n_rep)
    summed = pieces_ref[0].astype(jnp.float32)
    for j in range(1, n_rep):
        summed = summed + pieces_ref[j].astype(jnp.float32)
    summed = summed * (1.0 / n_rep)
    own_mean_ref[...] = summed
    all_mean_ref[piece(rep)] = summed
    start_all(lambda j: spread_copy(j, rep), 1, n_rep)

    def arrived(c, _):
        pltpu.make_async_remote_copy(
            src_ref=nm_ref.at[ds(peer, rows), ds(c, cw)],
            dst_ref=nm_ref.at[ds(peer, rows), ds(c, cw)],
            send_sem=ag_send.at[c],
            recv_sem=ag_recv.at[c],
            device_id={"tp": peer},
            device_id_type=MESH,
        ).wait_recv()
        part = nm_ref[ds(peer, rows), ds(c, cw)]

        def one(t, _):
            acc_ref[ds(peer, rows), ds(t, tile)] += dot(part, w_ref[ds(c, cw), ds(t, tile)])
            return 0

        lax.fori_loop(0, total // tile, one, 0)
        return 0

    lax.fori_loop(0, chunks, arrived, 0)

    cosine, sine = cos_ref[...], sin_ref[...]

    def rope_head(source, target, index):
        vector = acc_ref[:, ds(source, HEAD_SIZE)]
        target[:, ds(index, HEAD_SIZE)] = (
            vector * cosine + pltpu.roll(vector, HEAD_SIZE // 2, 1) * sine
        ).astype(jnp.bfloat16)

    heads_q, heads_kv = qw // HEAD_SIZE, kw // HEAD_SIZE
    for h in range(heads_q):
        rope_head(h, q_ref, h)
    for h in range(heads_kv):
        rope_head(heads_q + h, k_ref, h)
    v_ref[...] = acc_ref[:, pl.ds(qw + kw, kw)].astype(jnp.bfloat16)

    sequence = 2 * rows
    group = heads_q // heads_kv
    scale = HEAD_SIZE ** (-0.5)

    def reverse(gradient, block):
        c = cosine[block * rows : (block + 1) * rows]
        s = sine[block * rows : (block + 1) * rows]
        return (gradient * c - pltpu.roll(gradient, HEAD_SIZE // 2, 1) * s).astype(jnp.bfloat16)

    def kv_head(g, _):
        grad_k = [None, None]
        grad_v = [None, None]
        for r in range(group):
            head = ds(g * group + r, HEAD_SIZE)
            for b in range(2):
                keys = (b + 1) * rows
                block = pl.ds(b * rows, rows)
                query = q_ref[block, head]
                out_grad = go_ref[block, head]
                key = k_ref[pl.ds(0, keys), ds(g, HEAD_SIZE)]
                value = v_ref[pl.ds(0, keys), ds(g, HEAD_SIZE)]
                scores = dot(query, key, NT) * scale
                row = lax.broadcasted_iota(jnp.int32, scores.shape, 0) + b * rows
                col = lax.broadcasted_iota(jnp.int32, scores.shape, 1)
                scores = jnp.where(col <= row, scores, -jnp.inf)
                powers = jnp.exp(scores - jnp.max(scores, axis=-1, keepdims=True))
                prob = powers * (1.0 / jnp.sum(powers, axis=-1, keepdims=True))
                grad_prob = dot(out_grad, value, NT)
                inner = jnp.sum(grad_prob * prob, axis=-1, keepdims=True)
                score_low = (prob * (grad_prob - inner) * scale).astype(jnp.bfloat16)
                dq_ref[block, head] = reverse(dot(score_low, key), b)
                part_v = dot(prob.astype(jnp.bfloat16), out_grad, TN)
                part_k = dot(score_low, query, TN)
                for j in range(b + 1):
                    pv = part_v[j * rows : (j + 1) * rows]
                    pk = part_k[j * rows : (j + 1) * rows]
                    grad_v[j] = pv if grad_v[j] is None else grad_v[j] + pv
                    grad_k[j] = pk if grad_k[j] is None else grad_k[j] + pk
        for j in range(2):
            block = pl.ds(j * rows, rows)
            dk_ref[block, ds(g, HEAD_SIZE)] = reverse(grad_k[j], j)
            dv_ref[block, ds(g, HEAD_SIZE)] = grad_v[j].astype(jnp.bfloat16)
        return 0

    lax.fori_loop(0, heads_kv, kv_head, 0)

    normed_ref[...] = nm_ref[...]
    wait_recv_all(lambda j: spread_copy(j, lax.rem(rep + n_rep - j, n_rep)), 1, n_rep)
    mean_ref[...] = all_mean_ref[...]
    wait_send_all(gather_copy, 0, chunks)
    wait_send_all(scatter_copy, 1, n_rep)
    wait_send_all(lambda j: spread_copy(j, rep), 1, n_rep)


def pair_body(
    n_rep,
    tokens,
    norm_gain,
    w_query,
    key_weight,
    value_weight,
    attention_gradient,
    global_fragment,
    momentum,
    local_fragment,
):
    rows, width = tokens.shape[1:]
    sequence = 2 * rows
    weight_q, weight_k, weight_v = w_query[0], key_weight[0], value_weight[0]
    qw, kw = weight_q.shape[1], weight_k.shape[1]
    total = qw + 2 * kw
    frag_rows = local_fragment.shape[1]
    piece_rows = 16
    piece_cols = width * frag_rows // piece_rows // n_rep
    chunks = 6
    bf16, f32 = jnp.bfloat16, jnp.float32
    cosine, sine = host_tables(sequence, HEAD_SIZE)
    vmem = pl.BlockSpec(memory_space=pltpu.VMEM)
    anyspace = pl.BlockSpec(memory_space=pl.ANY)
    normed, dq, dk, dv, mean_local = pl.pallas_call(
        functools.partial(front_kernel, n_rep, chunks, 512),
        out_shape=(
            jax.ShapeDtypeStruct((sequence, width), bf16),
            jax.ShapeDtypeStruct((sequence, qw), bf16),
            jax.ShapeDtypeStruct((sequence, kw), bf16),
            jax.ShapeDtypeStruct((sequence, kw), bf16),
            jax.ShapeDtypeStruct((frag_rows, width), f32),
        ),
        in_specs=[vmem, vmem, anyspace, anyspace, anyspace, vmem, vmem, vmem, anyspace],
        out_specs=(vmem,) * 5,
        scratch_shapes=[
            pltpu.VMEM((width, total), bf16),
            pltpu.VMEM((sequence, width), bf16),
            pltpu.VMEM((sequence, total), f32),
            pltpu.VMEM((sequence, qw), bf16),
            pltpu.VMEM((sequence, kw), bf16),
            pltpu.VMEM((sequence, kw), bf16),
            pltpu.VMEM((n_rep, piece_rows, piece_cols), bf16),
            pltpu.VMEM((piece_rows, piece_cols), f32),
            pltpu.VMEM((frag_rows, width), f32),
            pltpu.SemaphoreType.DMA((3,)),
            pltpu.SemaphoreType.DMA((chunks,)),
            pltpu.SemaphoreType.DMA((chunks,)),
            pltpu.SemaphoreType.DMA((n_rep,)),
            pltpu.SemaphoreType.DMA((n_rep,)),
            pltpu.SemaphoreType.DMA((n_rep,)),
            pltpu.SemaphoreType.DMA((n_rep,)),
            pltpu.SemaphoreType.DMA,
        ],
        compiler_params=pltpu.CompilerParams(
            collective_id=0, has_side_effects=True, vmem_limit_bytes=40 * 1024 * 1024
        ),
    )(
        tokens[0],
        norm_gain,
        weight_q,
        weight_k,
        weight_v,
        attention_gradient[0],
        cosine,
        sine,
        local_fragment[0],
    )
    me = lax.axis_index("tp")
    swap = [(0, 1), (1, 0)]

    def half(array, which):
        return lax.dynamic_slice_in_dim(array, which * rows, rows, 0)

    def share(which, low, high):
        partial_value = dot(half(dq, which), weight_q[low:high], NT)
        partial_value = partial_value + dot(half(dk, which), weight_k[low:high], NT)
        partial_value = partial_value + dot(half(dv, which), weight_v[low:high], NT)
        return partial_value.astype(bf16)

    cuts = 2
    step = width // cuts
    away = [share(1 - me, c * step, (c + 1) * step) for c in range(cuts)]
    landed = [lax.ppermute(piece, "tp", swap) for piece in away]
    here = share(me, 0, width)
    far = jnp.concatenate(away, axis=1)
    gain_partial = (
        jnp.sum(
            far.astype(f32) * half(normed, 1 - me).astype(f32)
            + here.astype(f32) * half(normed, me).astype(f32),
            axis=0,
            keepdims=True,
        )
        / norm_gain
    )
    gains_gradient = gain_partial + lax.ppermute(gain_partial, "tp", swap)
    grad_wq = dot(normed, dq, TN).astype(bf16)
    grad_wk = dot(normed, dk, TN).astype(bf16)
    grad_wv = dot(normed, dv, TN).astype(bf16)
    mean_delta = global_fragment - mean_local
    new_momentum = outer_momentum * momentum + mean_delta
    new_global = global_fragment - outer_rate * (mean_delta + outer_momentum * new_momentum)
    summed_rows = here.astype(f32) + jnp.concatenate(landed, axis=1).astype(f32)
    widened_rows = tokens[0].astype(f32)
    inverse_norm = lax.rsqrt(
        jnp.mean(widened_rows * widened_rows, axis=-1, keepdims=True) + epsilon
    )
    normalized_input = widened_rows * inverse_norm
    scaled_rows = summed_rows * norm_gain
    gradient_rows = (
        inverse_norm
        * (
            scaled_rows
            - normalized_input * jnp.mean(scaled_rows * normalized_input, axis=-1, keepdims=True)
        )
    ).astype(bf16)
    return (
        grad_wq[None],
        grad_wk[None],
        grad_wv[None],
        gains_gradient,
        gradient_rows[None],
        new_global,
        new_momentum,
    )


def solution(mesh):
    placed = (
        P("rep", "tp", None),
        P("rep", None),
        P("rep", None, "tp"),
        P("rep", None, "tp"),
        P("rep", None, "tp"),
        P("rep", None, "tp"),
        P("tp", None),
        P("tp", None),
        P("rep", "tp", None),
    )
    paired = mesh.shape["tp"] == 2
    chosen = functools.partial(pair_body, mesh.shape["rep"]) if paired else body
    return jax.shard_map(
        chosen,
        mesh=mesh,
        in_specs=placed,
        out_specs=(
            P("rep", None, "tp"),
            P("rep", None, "tp"),
            P("rep", None, "tp"),
            P("rep", None),
            P("rep", "tp", None),
            P("tp", None),
            P("tp", None),
        ),
        check_vma=False,
    )
```

profile of v0, /device:TPU:0, one launch (start us, length us, event | category | flops | bytes accessed | tf_op | source)
XLA Modules:
  0.0 81.7 jit_solution(13407773457854130350)
XLA Ops:
  0.6 0.0 copy-start
  0.7 1.9 %copy-done = bf16[1,3072,512]{2,1,0:T(8,128)(2,1)S(1)} copy-done((bf16[1,3072,512]{2,1,0:T(8,128)(2,1)S(1)}, bf16[1,3072,512]{2,1,0:T(8,128)(2,1)}, u32[]{:S(2)}) %copy-start) | copy-done | bytes 3145752
  2.5 0.0 copy-start.2
  2.5 1.9 %copy-done.2 = bf16[1,3072,512]{2,1,0:T(8,128)(2,1)S(1)} copy-done((bf16[1,3072,512]{2,1,0:T(8,128)(2,1)S(1)}, bf16[1,3072,512]{2,1,0:T(8,128)(2,1)}, u32[]{:S(2)}) %copy-start.2) | copy-done | bytes 3145752
  4.4 0.0 copy-start.4
  4.4 1.1 %copy-done.4 = bf16[1,128,3072]{2,1,0:T(8,128)(2,1)S(1)} copy-done((bf16[1,128,3072]{2,1,0:T(8,128)(2,1)S(1)}, bf16[1,128,3072]{2,1,0:T(8,128)(2,1)}, u32[]{:S(2)}) %copy-start.4) | copy-done | bytes 786456
  5.6 0.0 copy-start.8
  5.6 1.0 %copy-done.8 = bf16[1,256,1024]{2,1,0:T(8,128)(2,1)S(1)} copy-done((bf16[1,256,1024]{2,1,0:T(8,128)(2,1)S(1)}, bf16[1,256,1024]{2,1,0:T(8,128)(2,1)}, u32[]{:S(2)}) %copy-start.8) | copy-done | bytes 524312
  6.6 0.0 copy-start.9
  6.6 1.0 %copy-done.9 = bf16[1,64,3072]{2,1,0:T(8,128)(2,1)S(1)} copy-done((bf16[1,64,3072]{2,1,0:T(8,128)(2,1)S(1)}, bf16[1,64,3072]{2,1,0:T(8,128)(2,1)}, u32[]{:S(2)}) %copy-start.9) | copy-done | bytes 393240
  7.6 0.0 copy-start.10
  7.6 0.7 copy-done.10
  8.3 0.0 copy-start.12
  8.3 0.9 %copy-done.12 = f32[256,128]{1,0:T(8,128)S(1)} copy-done((f32[256,128]{1,0:T(8,128)S(1)}, f32[256,128]{1,0:T(8,128)}, u32[]{:S(2)}) %copy-start.12) | copy-done | bytes 131096
  9.2 0.0 copy-start.13
  9.2 0.9 %copy-done.13 = f32[256,128]{1,0:T(8,128)S(1)} copy-done((f32[256,128]{1,0:T(8,128)S(1)}, f32[256,128]{1,0:T(8,128)}, u32[]{:S(2)}) %copy-start.13) | copy-done | bytes 131096
  10.1 0.0 copy-start.14
  10.1 36.0 %shard_map.162 = (bf16[256,3072]{1,0:T(8,128)(2,1)S(1)}, bf16[256,1024]{1,0:T(8,128)(2,1)S(1)}, bf16[256,512]{1,0:T(8,128)(2,1)S(1)}, bf16[256,512]{1,0:T(8,128)(2,1)S(1)}, f32[64,3072]{1,0:T(8,128)S(1)}) custom-call(bf16[128,3072]{1,0:T(8,128)(2,1)S(1)} %bitcast.57, f32[1,3072]{1,0:T(1,128)S(1)} %copy-done.10, bf16[3072,1024]{1,0:T(8,128)(2,1)} %bitcast.62, ...), custom_call_target="tpu_custom_call" | custom-call | tf_op jit(solution)/shard_map/pallas_call | solution.py:505
  46.1 0.0 copy-start.6
  46.2 0.6 fusion.29
  46.8 0.0 copy-done.14
  46.8 1.2 %fusion.10 = f32[128,1536]{1,0:T(8,128)S(1)} fusion(f32[128,1536]{1,0:T(8,128)S(1)} %fusion.29, bf16[1,3072,1024]{2,1,0:T(8,128)(2,1)S(1)} %copy-done.14, bf16[256,1024]{1,0:T(8,128)(2,1)S(1)} %get-tuple-element.13, s32[]{:T(128)S(6)} %select_n.4), kind=kOutput, calls=%fused_computation.15 | convolution fusion | flops 402849792 | bytes 4980740 | tf_op jit(solution)/shard_map/dot_general | solution.py:212
  48.0 0.0 copy-done.6
  48.0 1.4 %fusion.16 = bf16[128,1536]{1,0:T(8,128)(2,1)} fusion(f32[128,1536]{1,0:T(8,128)S(1)} %fusion.10, bf16[1,3072,512]{2,1,0:T(8,128)(2,1)S(1)} %copy-done.2, bf16[256,512]{1,0:T(8,128)(2,1)S(1)} %get-tuple-element.15, s32[]{:T(128)S(6)} %select_n.4), kind=kOutput, calls=%fused_computation.19 | convolution fusion | flops 201719808 | bytes 2883588 | tf_op jit(solution)/shard_map/dot_general | solution.py:212
  49.4 0.5 collective-permute-start.1
  49.9 0.6 fusion.26
  50.6 1.2 %fusion.13 = f32[128,1536]{1,0:T(8,128)S(1)} fusion(f32[128,1536]{1,0:T(8,128)S(1)} %fusion.26, bf16[1,3072,1024]{2,1,0:T(8,128)(2,1)S(1)} %copy-done.14, bf16[256,1024]{1,0:T(8,128)(2,1)S(1)} %get-tuple-element.13, s32[]{:T(128)S(6)} %select_n.4), kind=kOutput, calls=%fused_computation.16 | convolution fusion | flops 402849792 | bytes 4980740 | tf_op jit(solution)/shard_map/dot_general | solution.py:212
  51.8 0.0 copy-start.5
  51.8 1.4 %fusion.17 = bf16[128,1536]{1,0:T(8,128)(2,1)} fusion(f32[128,1536]{1,0:T(8,128)S(1)} %fusion.13, bf16[1,3072,512]{2,1,0:T(8,128)(2,1)S(1)} %copy-done.2, bf16[256,512]{1,0:T(8,128)(2,1)S(1)} %get-tuple-element.15, s32[]{:T(128)S(6)} %select_n.4), kind=kOutput, calls=%fused_computation.20 | convolution fusion | flops 201719808 | bytes 2883588 | tf_op jit(solution)/shard_map/dot_general | solution.py:212
  53.2 1.5 %collective-permute-start.2 = (bf16[128,1536]{1,0:T(8,128)(2,1)}, bf16[128,1536]{1,0:T(8,128)(2,1)}, u32[]{:S(2)}, u32[]{:S(2)}) collective-permute-start(bf16[128,1536]{1,0:T(8,128)(2,1)} %fusion.17), channel_id=1, source_target_pairs={{0,1},{1,0},{2,3},{3,2},{4,5},{5,4},{6,7},{7,6},{8,9},{9,8},{10,11... | collective-permute-start | bytes 1179656 | tf_op jit(solution)/shard_map/ppermute | solution.py:564
  54.7 0.0 copy-done.5
  54.7 0.2 fusion.24
  55.0 2.7 %fusion = bf16[1,3072,512]{2,1,0:T(8,128)(2,1)} fusion(bf16[256,3072]{1,0:T(8,128)(2,1)S(1)} %get-tuple-element.12, bf16[256,512]{1,0:T(8,128)(2,1)S(1)} %get-tuple-element.14), kind=kOutput, calls=%fused_computation.3 | convolution fusion | flops 806879232 | bytes 4980736 | tf_op jit(solution)/shard_map/dot_general | solution.py:212
  57.7 2.7 %fusion.1 = bf16[1,3072,512]{2,1,0:T(8,128)(2,1)} fusion(bf16[256,3072]{1,0:T(8,128)(2,1)S(1)} %get-tuple-element.12, bf16[256,512]{1,0:T(8,128)(2,1)S(1)} %get-tuple-element.15), kind=kOutput, calls=%fused_computation.4 | convolution fusion | flops 806879232 | bytes 4980736 | tf_op jit(solution)/shard_map/dot_general | solution.py:212
  60.3 4.5 %convert_bitcast_fusion = bf16[1,3072,1024]{2,1,0:T(8,128)(2,1)} fusion(bf16[256,3072]{1,0:T(8,128)(2,1)S(1)} %get-tuple-element.12, bf16[256,1024]{1,0:T(8,128)(2,1)S(1)} %get-tuple-element.13), kind=kOutput, calls=%fused_computation | convolution fusion | flops 1613758464 | bytes 8388608 | tf_op jit(solution)/shard_map/dot_general | solution.py:212
  64.9 0.0 copy-start.7
  64.9 0.0 copy-start.15
  64.9 0.0 copy-start.16
  64.9 5.1 %fusion.36 = f32[128,3072]{1,0:T(8,128)S(1)} fusion(bf16[256,1024]{1,0:T(8,128)(2,1)S(1)} %get-tuple-element.13, s32[]{:T(128)S(6)} %select_n.5, bf16[1,3072,1024]{2,1,0:T(8,128)(2,1)} %param.13), kind=kOutput, calls=%fused_computation.46 | convolution fusion | flops 805306368 | bytes 8126468 | tf_op jit(solution)/shard_map/dot_general | solution.py:212
  70.0 0.0 copy-done.7
  70.0 0.0 copy-done.15
  70.0 0.0 copy-done.16
  70.0 0.0 copy-start.1
  70.0 1.4 %multiply_subtract_fusion = (f32[64,3072]{1,0:T(8,128)}, f32[64,3072]{1,0:T(8,128)}) fusion(f32[64,3072]{1,0:T(8,128)S(1)} %copy-done.15, f32[64,3072]{1,0:T(8,128)S(1)} %copy-done.16, f32[64,3072]{1,0:T(8,128)S(1)} %copy-done.7), kind=kLoop, calls=%fused_computation.44 | loop fusion | flops 1376256 | bytes 3932160 | tf_op jit(solution)/shard_map/sub | solution.py:582
  71.4 1.1 %copy-done.1 = bf16[1,3072,512]{2,1,0:T(8,128)(2,1)S(1)} copy-done((bf16[1,3072,512]{2,1,0:T(8,128)(2,1)S(1)}, bf16[1,3072,512]{2,1,0:T(8,128)(2,1)}, u32[]{:S(2)}) %copy-start.1) | copy-done | bytes 3145752
  72.5 0.0 copy-start.3
  72.5 0.0 copy-start.11
  72.5 1.2 %convolution_add_fusion.1 = f32[128,3072]{1,0:T(8,128)S(1)} fusion(f32[128,3072]{1,0:T(8,128)S(1)} %fusion.36, bf16[256,512]{1,0:T(8,128)(2,1)S(1)} %get-tuple-element.14, s32[]{:T(128)S(6)} %select_n.5, bf16[1,3072,512]{2,1,0:T(8,128)(2,1)S(1)} %copy-done.1), kind=kOutput, calls=%fused_computation.6 | convolution fusion | flops 403046400 | bytes 6422532 | tf_op jit(solution)/shard_map/dot_general | solution.py:212
  73.7 0.0 collective-permute-done.1
  73.7 0.0 collective-permute-done.2
  73.7 0.7 copy-done.3
  74.4 0.0 copy-done.11
  74.4 2.9 %fusion.20 = (f32[128]{0:T(128)S(1)}, f32[3072]{0:T(1024)S(1)}, f32[128,3072]{1,0:T(8,128)S(1)}) fusion(f32[3072]{0:T(1024)S(1)} %bitcast.60, f32[128]{0:T(128)S(1)} %add_rsqrt_fusion, bf16[128,1536]{1,0:T(8,128)(2,1)} %collective-permute-done.2, bf16[128,1536]{1,0:T(8,128)(2,1)} %collective-permute-done.1, bf16[1,128,3072]{2,1,0:T(8,128)(2,1)S(1)} %copy-done.5, ...), kind=kOutput, calls=%fused_computation.25 | convolution fusion | flops 411693952 | bytes 10381824 | tf_op jit(solution)/shard_map/dot_general | solution.py:212
  77.3 0.6 collective-permute-start
  77.9 2.5 %fusion.35 = bf16[1,128,3072]{2,1,0:T(8,128)(2,1)} fusion(f32[128,3072]{1,0:T(8,128)S(1)} %get-tuple-element.21, f32[128]{0:T(128)S(1)} %broadcast_multiply_fusion, f32[3072]{0:T(1024)S(1)} %bitcast.61, f32[128]{0:T(128)S(1)} %add_rsqrt_fusion, bf16[128,1536]{1,0:T(8,128)(2,1)} %collective-permute-done.2, bf16[128,1536]{1,0:T(8,128)(2,1)} %collective-permute-done.1, ...), kind=kLoop, calls=%fused_computation.42 | loop fusion | flops 4718592 | bytes 3945472 | tf_op jit(solution)/shard_map/broadcast_in_dim | solution.py:602
  80.4 0.7 collective-permute-done
  81.1 0.6 add.68
  (3 shorter events, 0.0 us)
Async XLA Ops:
  0.6 1.9 %copy-start = (bf16[1,3072,512]{2,1,0:T(8,128)(2,1)S(1)}, bf16[1,3072,512]{2,1,0:T(8,128)(2,1)}, u32[]{:S(2)}) copy-start(bf16[1,3072,512]{2,1,0:T(8,128)(2,1)} %param.14) | copy-start | bytes 9437188
  2.5 1.9 %copy-start.2 = (bf16[1,3072,512]{2,1,0:T(8,128)(2,1)S(1)}, bf16[1,3072,512]{2,1,0:T(8,128)(2,1)}, u32[]{:S(2)}) copy-start(bf16[1,3072,512]{2,1,0:T(8,128)(2,1)} %param.15) | copy-start | bytes 9437188
  4.4 1.1 %copy-start.4 = (bf16[1,128,3072]{2,1,0:T(8,128)(2,1)S(1)}, bf16[1,128,3072]{2,1,0:T(8,128)(2,1)}, u32[]{:S(2)}) copy-start(bf16[1,128,3072]{2,1,0:T(8,128)(2,1)} %param.11) | copy-start | bytes 2359300
  5.6 1.0 %copy-start.8 = (bf16[1,256,1024]{2,1,0:T(8,128)(2,1)S(1)}, bf16[1,256,1024]{2,1,0:T(8,128)(2,1)}, u32[]{:S(2)}) copy-start(bf16[1,256,1024]{2,1,0:T(8,128)(2,1)} %param.16) | copy-start | bytes 1572868
  6.6 1.0 %copy-start.9 = (bf16[1,64,3072]{2,1,0:T(8,128)(2,1)S(1)}, bf16[1,64,3072]{2,1,0:T(8,128)(2,1)}, u32[]{:S(2)}) copy-start(bf16[1,64,3072]{2,1,0:T(8,128)(2,1)} %param.19) | copy-start | bytes 1179652
  7.6 0.7 copy-start.10
  8.3 0.9 %copy-start.12 = (f32[256,128]{1,0:T(8,128)S(1)}, f32[256,128]{1,0:T(8,128)}, u32[]{:S(2)}) copy-start(f32[256,128]{1,0:T(8,128)} %constant.28.clone.cos_ref) | copy-start | bytes 393220
  9.2 0.9 %copy-start.13 = (f32[256,128]{1,0:T(8,128)S(1)}, f32[256,128]{1,0:T(8,128)}, u32[]{:S(2)}) copy-start(f32[256,128]{1,0:T(8,128)} %constant.29.clone.sin_ref) | copy-start | bytes 393220
  10.1 36.7 %copy-start.14 = (bf16[1,3072,1024]{2,1,0:T(8,128)(2,1)S(1)}, bf16[1,3072,1024]{2,1,0:T(8,128)(2,1)}, u32[]{:S(2)}) copy-start(bf16[1,3072,1024]{2,1,0:T(8,128)(2,1)} %param.13) | copy-start | bytes 18874372
  46.1 1.9 %copy-start.6 = (f32[64,3072]{1,0:T(8,128)}, f32[64,3072]{1,0:T(8,128)S(1)}, u32[]{:S(2)}) copy-start(f32[64,3072]{1,0:T(8,128)S(1)} %get-tuple-element.16) | copy-start | bytes 2359300
  49.4 24.2 %collective-permute-start.1 = (bf16[128,1536]{1,0:T(8,128)(2,1)}, bf16[128,1536]{1,0:T(8,128)(2,1)}, u32[]{:S(2)}, u32[]{:S(2)}) collective-permute-start(bf16[128,1536]{1,0:T(8,128)(2,1)} %fusion.16), channel_id=1, source_target_pairs={{0,1},{1,0},{2,3},{3,2},{4,5},{5,4},{6,7},{7,6},{8,9},{9,8},{10,11... | collective-permute-start | bytes 1179656 | tf_op jit(solution)/shard_map/ppermute | solution.py:564
  51.8 2.9 %copy-start.5 = (bf16[1,128,3072]{2,1,0:T(8,128)(2,1)S(1)}, bf16[1,128,3072]{2,1,0:T(8,128)(2,1)}, u32[]{:S(2)}) copy-start(bf16[1,128,3072]{2,1,0:T(8,128)(2,1)} %param.11) | copy-start | bytes 2359300
  53.2 20.5 %collective-permute-start.2 = (bf16[128,1536]{1,0:T(8,128)(2,1)}, bf16[128,1536]{1,0:T(8,128)(2,1)}, u32[]{:S(2)}, u32[]{:S(2)}) collective-permute-start(bf16[128,1536]{1,0:T(8,128)(2,1)} %fusion.17), channel_id=1, source_target_pairs={{0,1},{1,0},{2,3},{3,2},{4,5},{5,4},{6,7},{7,6},{8,9},{9,8},{10,11... | collective-permute-start | bytes 1179656 | tf_op jit(solution)/shard_map/ppermute | solution.py:564
  64.9 5.1 %copy-start.7 = (f32[64,3072]{1,0:T(8,128)S(1)}, f32[64,3072]{1,0:T(8,128)}, u32[]{:S(2)}) copy-start(f32[64,3072]{1,0:T(8,128)} %copy-done.6) | copy-start | bytes 2359300
  64.9 5.1 %copy-start.15 = (f32[64,3072]{1,0:T(8,128)S(1)}, f32[64,3072]{1,0:T(8,128)}, u32[]{:S(2)}) copy-start(f32[64,3072]{1,0:T(8,128)} %param.17) | copy-start | bytes 2359300
  64.9 5.1 %copy-start.16 = (f32[64,3072]{1,0:T(8,128)S(1)}, f32[64,3072]{1,0:T(8,128)}, u32[]{:S(2)}) copy-start(f32[64,3072]{1,0:T(8,128)} %param.18) | copy-start | bytes 2359300
  70.0 2.5 %copy-start.1 = (bf16[1,3072,512]{2,1,0:T(8,128)(2,1)S(1)}, bf16[1,3072,512]{2,1,0:T(8,128)(2,1)}, u32[]{:S(2)}) copy-start(bf16[1,3072,512]{2,1,0:T(8,128)(2,1)} %param.14) | copy-start | bytes 9437188
  72.5 1.9 %copy-start.3 = (bf16[1,3072,512]{2,1,0:T(8,128)(2,1)S(1)}, bf16[1,3072,512]{2,1,0:T(8,128)(2,1)}, u32[]{:S(2)}) copy-start(bf16[1,3072,512]{2,1,0:T(8,128)(2,1)} %param.15) | copy-start | bytes 9437188
  72.5 1.9 %copy-start.11 = (f32[1,3072]{1,0:T(1,128)S(1)}, f32[1,3072]{1,0:T(1,128)}, u32[]{:S(2)}) copy-start(f32[1,3072]{1,0:T(1,128)} %gain_ref.1) | copy-start | bytes 36868
  77.3 3.8 %collective-permute-start = (f32[1,3072]{1,0:T(1,128)S(1)}, f32[1,3072]{1,0:T(1,128)S(1)}, u32[]{:S(2)}, u32[]{:S(2)}) collective-permute-start(f32[1,3072]{1,0:T(1,128)S(1)} %div.9), channel_id=1, source_target_pairs={{0,1},{1,0},{2,3},{3,2},{4,5},{5,4},{6,7},{7,6},{8,9},{9,8},{10,11... | collective-permute-start | bytes 36872 | tf_op jit(solution)/shard_map/ppermute | solution.py:576
where the time goes:
time: 82.2 us; the launch traced here: 81.7 us
  Pallas kernels  36 us (44%)
  matrix products  25.5 us (31%)
  local copies, waits for them, and re-layouts  11.2 us (14%)
  other arithmetic  4.81 us (6%)
  starting transfers between devices  2.6 us (3%)
    pallas_call x1, Pallas kernels, pair_body(): pl.pallas_call(functools.partial(front_kernel, n_rep, chunks, 512), out_s...  36 us
    dot_general x12, matrix products, dot(): return lax.dot_general(a, b, dims, preferred_element_type=jnp.float32)  25.5 us
    unnamed x34, local copies, waits for them, and re-layouts  11.2 us
    broadcast_in_dim x1, other arithmetic, pair_body(): gradient_rows[None]  2.53 us
    ppermute x2, starting transfers between devices, pair_body(): landed = [lax.ppermute(piece, 'tp', swap) for piece in away]  2.03 us
  transfers between devices with their start and end apart: 3, of which 1 were waited for; matrix products, arithmetic and copies ran while one was open for 29% of the time, Pallas kernels for 0%

commit v1 on v0

--- a/solution.py
+++ b/solution.py
@@ -17,6 +17,7 @@
 rope_base = 500000.0
 outer_rate = 0.7
 outer_momentum = 0.9
+LOG2_E = 1.4426950408889634
 
 
 def rope_tables(sequence_length, width):
@@ -231,30 +232,37 @@
     n_rep,
     chunks,
     tile,
-    tokens_ref,
-    gain_ref,
+    tokens_hbm,
+    gain_hbm,
     wq_hbm,
     wk_hbm,
     wv_hbm,
+    go_hbm,
+    cos_hbm,
+    sin_hbm,
+    local_hbm,
+    x_ref,
+    nm_ref,
+    d_ref,
+    here_ref,
+    far_hbm,
+    gain_part_ref,
+    mean_ref,
+    gain_ref,
     go_ref,
     cos_ref,
     sin_ref,
-    local_hbm,
-    normed_ref,
-    dq_ref,
-    dk_ref,
-    dv_ref,
-    mean_ref,
     w_ref,
-    nm_ref,
     acc_ref,
     q_ref,
     k_ref,
     v_ref,
+    far_ref,
     pieces_ref,
     own_mean_ref,
-    all_mean_ref,
+    in_sems,
     w_sems,
+    far_sems,
     ag_send,
     ag_recv,
     fr_send,
@@ -262,11 +270,13 @@
     fg_send,
     fg_recv,
     own_sem,
+    go_sem,
 ):
     me = lax.axis_index("tp")
     peer = 1 - me
     rep = lax.axis_index("rep")
-    rows, width = tokens_ref.shape
+    side = lax.rem(rep, 2)
+    rows, width = x_ref.shape
     qw, kw = wq_hbm.shape[1], wk_hbm.shape[1]
     total = qw + 2 * kw
     cw = width // chunks
@@ -282,13 +292,25 @@
         return 0
 
     lax.fori_loop(1, n_rep, greet, 0)
-    weight_copies = [
-        pltpu.make_async_copy(wq_hbm, w_ref.at[:, pl.ds(0, qw)], w_sems.at[0]),
-        pltpu.make_async_copy(wk_hbm, w_ref.at[:, pl.ds(qw, kw)], w_sems.at[1]),
-        pltpu.make_async_copy(wv_hbm, w_ref.at[:, pl.ds(qw + kw, kw)], w_sems.at[2]),
+    first_copies = [
+        pltpu.make_async_copy(tokens_hbm, x_ref, in_sems.at[0]),
+        pltpu.make_async_copy(gain_hbm, gain_ref, in_sems.at[1]),
     ]
-    for copy in weight_copies:
-        copy.start()
+    late_copies = [
+        pltpu.make_async_copy(cos_hbm, cos_ref, in_sems.at[2]),
+        pltpu.make_async_copy(sin_hbm, sin_ref, in_sems.at[3]),
+        pltpu.make_async_copy(go_hbm, go_ref, in_sems.at[4]),
+    ]
+    weight_copies = []
+    for source, offset in ((wq_hbm, 0), (wk_hbm, qw), (wv_hbm, qw + kw)):
+        for t in range(source.shape[1] // tile):
+            weight_copies.append(
+                pltpu.make_async_copy(
+                    source.at[:, pl.ds(t * tile, tile)],
+                    w_ref.at[:, pl.ds(offset + t * tile, tile)],
+                    w_sems.at[len(weight_copies)],
+                )
+            )
 
     def piece(owner):
         return (
@@ -297,12 +319,17 @@
         )
 
     own_piece = pltpu.make_async_copy(local_hbm.at[piece(rep)], pieces_ref.at[0], own_sem)
+    for copy in first_copies + weight_copies[:1] + late_copies[:2] + weight_copies[1:]:
+        copy.start()
     own_piece.start()
+    late_copies[2].start()
+    for copy in first_copies:
+        copy.wait()
 
     step = 16
 
     def norm_rows(i, _):
-        x = tokens_ref[ds(i, step), :].astype(jnp.float32)
+        x = x_ref[ds(i, step), :].astype(jnp.float32)
         inverse = lax.rsqrt(jnp.mean(x * x, axis=-1, keepdims=True) + epsilon)
         nm_ref[pl.ds(pl.multiple_of(me * rows + i * step, step), step), :] = (
             x * inverse * gain_ref[...]
@@ -337,7 +364,7 @@
     def spread_copy(j, owner):
         return pltpu.make_async_remote_copy(
             src_ref=own_mean_ref,
-            dst_ref=all_mean_ref.at[piece(owner)],
+            dst_ref=mean_ref.at[piece(owner)],
             send_sem=fg_send.at[j],
             recv_sem=fg_recv.at[j],
             device_id={"rep": lax.rem(rep + j, n_rep)},
@@ -365,28 +392,57 @@
 
         lax.fori_loop(low, high, one, 0)
 
-    start_all(gather_copy, 0, chunks)
+    @pl.when(side == 0)
+    def _():
+        start_all(gather_copy, 0, chunks)
+
     start_all(scatter_copy, 1, n_rep)
 
-    for copy in weight_copies:
+    for t, copy in enumerate(weight_copies):
         copy.wait()
-
-    def own_tile(t, _):
-        acc_ref[ds(me, rows), ds(t, tile)] = dot(nm_ref[ds(me, rows), :], w_ref[:, ds(t, tile)])
-        return 0
-
-    lax.fori_loop(0, total // tile, own_tile, 0)
+        acc_ref[ds(me, rows), pl.ds(t * tile, tile)] = dot(
+            nm_ref[ds(me, rows), :], w_ref[:, pl.ds(t * tile, tile)]
+        )
     acc_ref[ds(peer, rows), :] = jnp.zeros((rows, total), jnp.float32)
-
-    own_piece.wait()
-    wait_recv_all(scatter_copy, 1, n_rep)
-    summed = pieces_ref[0].astype(jnp.float32)
-    for j in range(1, n_rep):
-        summed = summed + pieces_ref[j].astype(jnp.float32)
-    summed = summed * (1.0 / n_rep)
-    own_mean_ref[...] = summed
-    all_mean_ref[piece(rep)] = summed
-    start_all(lambda j: spread_copy(j, rep), 1, n_rep)
+    for copy in late_copies:
+        copy.wait()
+
+    heads_q, heads_kv = qw // HEAD_SIZE, kw // HEAD_SIZE
+
+    def rope_rows(which):
+        block = ds(which, rows)
+        cosine, sine = cos_ref[block, :], sin_ref[block, :]
+
+        def rope_head(source, target, index):
+            vector = acc_ref[block, pl.ds(source * HEAD_SIZE, HEAD_SIZE)]
+            target[block, pl.ds(index * HEAD_SIZE, HEAD_SIZE)] = (
+                vector * cosine + pltpu.roll(vector, HEAD_SIZE // 2, 1) * sine
+            ).astype(jnp.bfloat16)
+
+        for h in range(heads_q):
+            rope_head(h, q_ref, h)
+        for h in range(heads_kv):
+            rope_head(heads_q + h, k_ref, h)
+        v_ref[block, :] = acc_ref[block, pl.ds(qw + kw, kw)].astype(jnp.bfloat16)
+
+    rope_rows(me)
+
+    def average_pieces():
+        own_piece.wait()
+        wait_recv_all(scatter_copy, 1, n_rep)
+        summed = pieces_ref[0].astype(jnp.float32)
+        for j in range(1, n_rep):
+            summed = summed + pieces_ref[j].astype(jnp.float32)
+        summed = (summed * (1.0 / n_rep)).astype(jnp.bfloat16)
+        own_mean_ref[...] = summed
+        mean_ref[piece(rep)] = summed
+        start_all(lambda j: spread_copy(j, rep), 1, n_rep)
+
+    @pl.when(side == 1)
+    def _():
+        pl.semaphore_wait(go_sem, 1)
+        start_all(gather_copy, 0, chunks)
+        average_pieces()
 
     def arrived(c, _):
         pltpu.make_async_remote_copy(
@@ -397,6 +453,13 @@
             device_id={"tp": peer},
             device_id_type=MESH,
         ).wait_recv()
+
+        @pl.when((side == 0) & (c == chunks - 2))
+        def _():
+            pl.semaphore_signal(
+                go_sem, inc=1, device_id={"rep": lax.rem(rep + 1, n_rep)}, device_id_type=MESH
+            )
+
         part = nm_ref[ds(peer, rows), ds(c, cw)]
 
         def one(t, _):
@@ -407,74 +470,134 @@
         return 0
 
     lax.fori_loop(0, chunks, arrived, 0)
-
-    cosine, sine = cos_ref[...], sin_ref[...]
-
-    def rope_head(source, target, index):
-        vector = acc_ref[:, ds(source, HEAD_SIZE)]
-        target[:, ds(index, HEAD_SIZE)] = (
-            vector * cosine + pltpu.roll(vector, HEAD_SIZE // 2, 1) * sine
-        ).astype(jnp.bfloat16)
-
-    heads_q, heads_kv = qw // HEAD_SIZE, kw // HEAD_SIZE
-    for h in range(heads_q):
-        rope_head(h, q_ref, h)
-    for h in range(heads_kv):
-        rope_head(heads_q + h, k_ref, h)
-    v_ref[...] = acc_ref[:, pl.ds(qw + kw, kw)].astype(jnp.bfloat16)
-
-    sequence = 2 * rows
+    rope_rows(peer)
+
     group = heads_q // heads_kv
     scale = HEAD_SIZE ** (-0.5)
+    key_pos = lax.broadcasted_iota(jnp.int32, (rows, rows), 0)
+    query_pos = lax.broadcasted_iota(jnp.int32, (rows, rows), 1)
+    bias = jnp.where(key_pos <= query_pos, 0.0, -jnp.inf).astype(jnp.float32)
+    bias = jnp.concatenate([bias] * group, axis=1)
 
     def reverse(gradient, block):
-        c = cosine[block * rows : (block + 1) * rows]
-        s = sine[block * rows : (block + 1) * rows]
+        c = cos_ref[block * rows : (block + 1) * rows]
+        s = sin_ref[block * rows : (block + 1) * rows]
         return (gradient * c - pltpu.roll(gradient, HEAD_SIZE // 2, 1) * s).astype(jnp.bfloat16)
 
     def kv_head(g, _):
+        @pl.when((side == 0) & (g == 1))
+        def _():
+            average_pieces()
+
         grad_k = [None, None]
         grad_v = [None, None]
-        for r in range(group):
-            head = ds(g * group + r, HEAD_SIZE)
-            for b in range(2):
-                keys = (b + 1) * rows
-                block = pl.ds(b * rows, rows)
-                query = q_ref[block, head]
-                out_grad = go_ref[block, head]
-                key = k_ref[pl.ds(0, keys), ds(g, HEAD_SIZE)]
-                value = v_ref[pl.ds(0, keys), ds(g, HEAD_SIZE)]
-                scores = dot(query, key, NT) * scale
-                row = lax.broadcasted_iota(jnp.int32, scores.shape, 0) + b * rows
-                col = lax.broadcasted_iota(jnp.int32, scores.shape, 1)
-                scores = jnp.where(col <= row, scores, -jnp.inf)
-                powers = jnp.exp(scores - jnp.max(scores, axis=-1, keepdims=True))
-                prob = powers * (1.0 / jnp.sum(powers, axis=-1, keepdims=True))
-                grad_prob = dot(out_grad, value, NT)
-                inner = jnp.sum(grad_prob * prob, axis=-1, keepdims=True)
-                score_low = (prob * (grad_prob - inner) * scale).astype(jnp.bfloat16)
-                dq_ref[block, head] = reverse(dot(score_low, key), b)
-                part_v = dot(prob.astype(jnp.bfloat16), out_grad, TN)
-                part_k = dot(score_low, query, TN)
-                for j in range(b + 1):
-                    pv = part_v[j * rows : (j + 1) * rows]
-                    pk = part_k[j * rows : (j + 1) * rows]
-                    grad_v[j] = pv if grad_v[j] is None else grad_v[j] + pv
-                    grad_k[j] = pk if grad_k[j] is None else grad_k[j] + pk
+        kv = ds(g, HEAD_SIZE)
+        for b in range(2):
+            keys = (b + 1) * rows
+            block = pl.ds(b * rows, rows)
+            heads = [ds(g * group + r, HEAD_SIZE) for r in range(group)]
+            query = jnp.concatenate([q_ref[block, head] for head in heads], axis=0)
+            out_grad = jnp.concatenate([go_ref[block, head] for head in heads], axis=0)
+            key = k_ref[pl.ds(0, keys), kv]
+            value = v_ref[pl.ds(0, keys), kv]
+            scores = dot(key, query, NT)
+            grad_prob = dot(value, out_grad, NT)
+            if b == 0:
+                scores = scores + bias
+            else:
+                scores = jnp.concatenate([scores[:rows], scores[rows:] + bias], axis=0)
+            highest = jnp.max(scores, axis=0, keepdims=True)
+            powers = jnp.exp2((scores - highest) * (scale * LOG2_E))
+            prob = powers * (1.0 / jnp.sum(powers, axis=0, keepdims=True))
+            inner = jnp.sum(grad_prob * prob, axis=0, keepdims=True)
+            score_low = (prob * (grad_prob - inner) * scale).astype(jnp.bfloat16)
+            grad_q = dot(score_low, key, TN)
+            for r, head in enumerate(heads):
+                d_ref[block, head] = reverse(grad_q[r * rows : (r + 1) * rows], b)
+            part_v = dot(prob.astype(jnp.bfloat16), out_grad)
+            part_k = dot(score_low, query)
+            for j in range(b + 1):
+                pv = part_v[j * rows : (j + 1) * rows]
+                pk = part_k[j * rows : (j + 1) * rows]
+                grad_v[j] = pv if grad_v[j] is None else grad_v[j] + pv
+                grad_k[j] = pk if grad_k[j] is None else grad_k[j] + pk
         for j in range(2):
             block = pl.ds(j * rows, rows)
-            dk_ref[block, ds(g, HEAD_SIZE)] = reverse(grad_k[j], j)
-            dv_ref[block, ds(g, HEAD_SIZE)] = grad_v[j].astype(jnp.bfloat16)
+            d_ref[block, ds(heads_q + g, HEAD_SIZE)] = reverse(grad_k[j], j)
+            d_ref[block, ds(heads_q + heads_kv + g, HEAD_SIZE)] = grad_v[j].astype(jnp.bfloat16)
         return 0
 
     lax.fori_loop(0, heads_kv, kv_head, 0)
 
-    normed_ref[...] = nm_ref[...]
+    def far_copy(t):
+        return pltpu.make_async_copy(
+            far_ref.at[:, ds(t, tile)], far_hbm.at[:, ds(t, tile)], far_sems.at[t]
+        )
+
+    def back(t, _):
+        both = jnp.concatenate([d_ref[ds(peer, rows), :], d_ref[ds(me, rows), :]], axis=0)
+        part = dot(both, w_ref[ds(t, tile), :], NT).astype(jnp.bfloat16)
+        cols = ds(t, tile)
+        far_ref[:, cols] = part[:rows]
+        here_ref[:, cols] = part[rows:]
+        wide = part.astype(jnp.float32)
+        products = wide[:rows] * nm_ref[ds(peer, rows), cols].astype(jnp.float32)
+        products += wide[rows:] * nm_ref[ds(me, rows), cols].astype(jnp.float32)
+        gain_part_ref[:, cols] = jnp.sum(products, axis=0, keepdims=True) / gain_ref[:, cols]
+        far_copy(t).start()
+        return 0
+
+    tiles = width // tile
+    lax.fori_loop(0, tiles, back, 0)
+
     wait_recv_all(lambda j: spread_copy(j, lax.rem(rep + n_rep - j, n_rep)), 1, n_rep)
-    mean_ref[...] = all_mean_ref[...]
     wait_send_all(gather_copy, 0, chunks)
     wait_send_all(scatter_copy, 1, n_rep)
     wait_send_all(lambda j: spread_copy(j, rep), 1, n_rep)
+    for t in range(tiles):
+        far_copy(t).wait()
+
+
+def weights_kernel(nm_ref, d_ref, mean_ref, global_ref, momentum_ref, gq_ref, gk_ref, gv_ref, ng_ref, nmom_ref):
+    i = pl.program_id(0)
+    wide = gq_ref.shape[0]
+    qw, kw = gq_ref.shape[1], gk_ref.shape[1]
+    grad = dot(nm_ref[:, ds(i, wide)], d_ref[...], TN).astype(jnp.bfloat16)
+    gq_ref[...] = grad[:, :qw]
+    gk_ref[...] = grad[:, qw : qw + kw]
+    gv_ref[...] = grad[:, qw + kw :]
+    held = global_ref[...]
+    mean_delta = held - mean_ref[:, ds(i, wide)].astype(jnp.float32)
+    new_momentum = outer_momentum * momentum_ref[...] + mean_delta
+    nmom_ref[...] = new_momentum
+    ng_ref[...] = held - outer_rate * (mean_delta + outer_momentum * new_momentum)
+
+
+def rows_kernel(x_ref, here_ref, gain_ref, landed_ref, gain_a_ref, gain_b_ref, out_ref, gain_out_ref):
+    i = pl.program_id(0)
+    count = landed_ref.shape[0]
+
+    @pl.when(i == 0)
+    def _():
+        gain_out_ref[...] = gain_a_ref[...] + gain_b_ref[...]
+
+    step = 16
+
+    def some(j, _):
+        block = pl.ds(pl.multiple_of(i * count + j * step, step), step)
+        part = ds(j, step)
+        x = x_ref[block, :].astype(jnp.float32)
+        inverse = lax.rsqrt(jnp.mean(x * x, axis=-1, keepdims=True) + epsilon)
+        xhat = x * inverse
+        scaled = (
+            here_ref[block, :].astype(jnp.float32) + landed_ref[part, :].astype(jnp.float32)
+        ) * gain_ref[...]
+        out_ref[part, :] = (
+            inverse * (scaled - xhat * jnp.mean(scaled * xhat, axis=-1, keepdims=True))
+        ).astype(jnp.bfloat16)
+        return 0
+
+    lax.fori_loop(0, count // step, some, 0)
 
 
 def pair_body(
@@ -498,32 +621,40 @@
     piece_rows = 16
     piece_cols = width * frag_rows // piece_rows // n_rep
     chunks = 6
+    tile = 512
     bf16, f32 = jnp.bfloat16, jnp.float32
     cosine, sine = host_tables(sequence, HEAD_SIZE)
     vmem = pl.BlockSpec(memory_space=pltpu.VMEM)
-    anyspace = pl.BlockSpec(memory_space=pl.ANY)
-    normed, dq, dk, dv, mean_local = pl.pallas_call(
-        functools.partial(front_kernel, n_rep, chunks, 512),
+    hbm = pl.BlockSpec(memory_space=pltpu.HBM)
+    x, normed, d, here, far, gain_partial, mean_local = pl.pallas_call(
+        functools.partial(front_kernel, n_rep, chunks, tile),
         out_shape=(
+            jax.ShapeDtypeStruct((rows, width), bf16),
             jax.ShapeDtypeStruct((sequence, width), bf16),
-            jax.ShapeDtypeStruct((sequence, qw), bf16),
-            jax.ShapeDtypeStruct((sequence, kw), bf16),
-            jax.ShapeDtypeStruct((sequence, kw), bf16),
-            jax.ShapeDtypeStruct((frag_rows, width), f32),
+            jax.ShapeDtypeStruct((sequence, total), bf16),
+            jax.ShapeDtypeStruct((rows, width), bf16),
+            jax.ShapeDtypeStruct((rows, width), bf16),
+            jax.ShapeDtypeStruct((1, width), f32),
+            jax.ShapeDtypeStruct((frag_rows, width), bf16),
         ),
-        in_specs=[vmem, vmem, anyspace, anyspace, anyspace, vmem, vmem, vmem, anyspace],
-        out_specs=(vmem,) * 5,
+        in_specs=[hbm] * 9,
+        out_specs=(vmem, vmem, vmem, vmem, hbm, vmem, vmem),
         scratch_shapes=[
+            pltpu.VMEM((1, width), f32),
+            pltpu.VMEM((sequence, qw), bf16),
+            pltpu.VMEM((sequence, HEAD_SIZE), f32),
+            pltpu.VMEM((sequence, HEAD_SIZE), f32),
             pltpu.VMEM((width, total), bf16),
-            pltpu.VMEM((sequence, width), bf16),
             pltpu.VMEM((sequence, total), f32),
             pltpu.VMEM((sequence, qw), bf16),
             pltpu.VMEM((sequence, kw), bf16),
             pltpu.VMEM((sequence, kw), bf16),
+            pltpu.VMEM((rows, width), bf16),
             pltpu.VMEM((n_rep, piece_rows, piece_cols), bf16),
-            pltpu.VMEM((piece_rows, piece_cols), f32),
-            pltpu.VMEM((frag_rows, width), f32),
-            pltpu.SemaphoreType.DMA((3,)),
+            pltpu.VMEM((piece_rows, piece_cols), bf16),
+            pltpu.SemaphoreType.DMA((5,)),
+            pltpu.SemaphoreType.DMA((total // tile,)),
+            pltpu.SemaphoreType.DMA((width // tile,)),
             pltpu.SemaphoreType.DMA((chunks,)),
             pltpu.SemaphoreType.DMA((chunks,)),
             pltpu.SemaphoreType.DMA((n_rep,)),
@@ -531,9 +662,10 @@
             pltpu.SemaphoreType.DMA((n_rep,)),
             pltpu.SemaphoreType.DMA((n_rep,)),
             pltpu.SemaphoreType.DMA,
+            pltpu.SemaphoreType.REGULAR,
         ],
         compiler_params=pltpu.CompilerParams(
-            collective_id=0, has_side_effects=True, vmem_limit_bytes=40 * 1024 * 1024
+            collective_id=0, has_side_effects=True, vmem_limit_bytes=48 * 1024 * 1024
         ),
     )(
         tokens[0],
@@ -546,54 +678,50 @@
         sine,
         local_fragment[0],
     )
-    me = lax.axis_index("tp")
     swap = [(0, 1), (1, 0)]
-
-    def half(array, which):
-        return lax.dynamic_slice_in_dim(array, which * rows, rows, 0)
-
-    def share(which, low, high):
-        partial_value = dot(half(dq, which), weight_q[low:high], NT)
-        partial_value = partial_value + dot(half(dk, which), weight_k[low:high], NT)
-        partial_value = partial_value + dot(half(dv, which), weight_v[low:high], NT)
-        return partial_value.astype(bf16)
-
-    cuts = 2
-    step = width // cuts
-    away = [share(1 - me, c * step, (c + 1) * step) for c in range(cuts)]
-    landed = [lax.ppermute(piece, "tp", swap) for piece in away]
-    here = share(me, 0, width)
-    far = jnp.concatenate(away, axis=1)
-    gain_partial = (
-        jnp.sum(
-            far.astype(f32) * half(normed, 1 - me).astype(f32)
-            + here.astype(f32) * half(normed, me).astype(f32),
-            axis=0,
-            keepdims=True,
-        )
-        / norm_gain
-    )
-    gains_gradient = gain_partial + lax.ppermute(gain_partial, "tp", swap)
-    grad_wq = dot(normed, dq, TN).astype(bf16)
-    grad_wk = dot(normed, dk, TN).astype(bf16)
-    grad_wv = dot(normed, dv, TN).astype(bf16)
-    mean_delta = global_fragment - mean_local
-    new_momentum = outer_momentum * momentum + mean_delta
-    new_global = global_fragment - outer_rate * (mean_delta + outer_momentum * new_momentum)
-    summed_rows = here.astype(f32) + jnp.concatenate(landed, axis=1).astype(f32)
-    widened_rows = tokens[0].astype(f32)
-    inverse_norm = lax.rsqrt(
-        jnp.mean(widened_rows * widened_rows, axis=-1, keepdims=True) + epsilon
-    )
-    normalized_input = widened_rows * inverse_norm
-    scaled_rows = summed_rows * norm_gain
-    gradient_rows = (
-        inverse_norm
-        * (
-            scaled_rows
-            - normalized_input * jnp.mean(scaled_rows * normalized_input, axis=-1, keepdims=True)
-        )
-    ).astype(bf16)
+    landed = lax.ppermute(far, "tp", swap)
+    gain_landed = lax.ppermute(gain_partial, "tp", swap)
+    wide = 256
+    columns = lambda size: pl.BlockSpec((size, wide), lambda i: (0, i))
+    grad_wq, grad_wk, grad_wv, new_global, new_momentum = pl.pallas_call(
+        weights_kernel,
+        grid=(width // wide,),
+        out_shape=(
+            jax.ShapeDtypeStruct((width, qw), bf16),
+            jax.ShapeDtypeStruct((width, kw), bf16),
+            jax.ShapeDtypeStruct((width, kw), bf16),
+            jax.ShapeDtypeStruct((frag_rows, width), f32),
+            jax.ShapeDtypeStruct((frag_rows, width), f32),
+        ),
+        in_specs=[vmem, vmem, vmem, columns(frag_rows), columns(frag_rows)],
+        out_specs=(
+            pl.BlockSpec((wide, qw), lambda i: (i, 0)),
+            pl.BlockSpec((wide, kw), lambda i: (i, 0)),
+            pl.BlockSpec((wide, kw), lambda i: (i, 0)),
+            columns(frag_rows),
+            columns(frag_rows),
+        ),
+        compiler_params=pltpu.CompilerParams(vmem_limit_bytes=16 * 1024 * 1024),
+        cost_estimate=pl.CostEstimate(
+            flops=2 * sequence * width * total, bytes_accessed=3 * width * total, transcendentals=0
+        ),
+    )(normed, d, mean_local, global_fragment, momentum)
+    count = 32
+    block = pl.BlockSpec((count, width), lambda i: (i, 0))
+    gradient_rows, gains_gradient = pl.pallas_call(
+        rows_kernel,
+        grid=(rows // count,),
+        out_shape=(
+            jax.ShapeDtypeStruct((rows, width), bf16),
+            jax.ShapeDtypeStruct((1, width), f32),
+        ),
+        in_specs=[vmem, vmem, vmem, block, vmem, vmem],
+        out_specs=(block, pl.BlockSpec((1, width), lambda i: (0, 0))),
+        compiler_params=pltpu.CompilerParams(vmem_limit_bytes=8 * 1024 * 1024),
+        cost_estimate=pl.CostEstimate(
+            flops=12 * rows * width, bytes_accessed=4 * rows * width, transcendentals=0
+        ),
+    )(x, here, norm_gain, landed, gain_partial, gain_landed)
     return (
         grad_wq[None],
         grad_wk[None],
@@ -617,7 +745,7 @@
         P("tp", None),
         P("rep", "tp", None),
     )
-    paired = mesh.shape["tp"] == 2
+    paired = mesh.shape["tp"] == 2 and mesh.shape["rep"] % 2 == 0
     chosen = functools.partial(pair_body, mesh.shape["rep"]) if paired else body
     return jax.shard_map(
         chosen,

time: 82.2 us -> 59.7 us (0.73)
  the two profiles are of different devices: /device:TPU:0 before, /device:TPU:1 now
where the time goes in v1:
time: 59.7 us; the launch traced here: 59.4 us
  Pallas kernels  49.8 us (83%)
  local copies, waits for them, and re-layouts  7.09 us (12%)
  starting transfers between devices  1.53 us (3%)
  between operations  0.66 us (1%)
    pallas_call x1, Pallas kernels, pair_body(): pl.pallas_call(functools.partial(front_kernel, n_rep, chunks, tile), out_...  38 us
    pallas_call x1, Pallas kernels, pair_body(): pl.pallas_call(weights_kernel, grid=(width // wide,), out_shape=(jax.Shap...  8.96 us
    unnamed x18, local copies, waits for them, and re-layouts  7.09 us
    pallas_call x1, Pallas kernels, pair_body(): pl.pallas_call(rows_kernel, grid=(rows // count,), out_shape=(jax.ShapeDt...  2.83 us
    ppermute x1, starting transfers between devices, pair_body(): landed = lax.ppermute(far, 'tp', swap)  1.31 us
  transfers between devices with their start and end apart: 2, of which 1 were waited for; matrix products, arithmetic and copies ran while one was open for 0% of the time, Pallas kernels for 15%

profile of v1, /device:TPU:1, one launch (start us, length us, event | category | flops | bytes accessed | tf_op | source)
XLA Modules:
  0.0 59.4 jit_solution(1917892000424254968)
XLA Ops:
  0.6 0.0 copy-start
  0.6 1.1 %copy-done = bf16[1,128,3072]{2,1,0:T(8,128)(2,1)S(1)} copy-done((bf16[1,128,3072]{2,1,0:T(8,128)(2,1)S(1)}, bf16[1,128,3072]{2,1,0:T(8,128)(2,1)}, u32[]{:S(2)}) %copy-start) | copy-done | bytes 786456
  1.8 0.0 copy-start.1
  1.8 1.0 %copy-done.1 = bf16[1,256,1024]{2,1,0:T(8,128)(2,1)S(1)} copy-done((bf16[1,256,1024]{2,1,0:T(8,128)(2,1)S(1)}, bf16[1,256,1024]{2,1,0:T(8,128)(2,1)}, u32[]{:S(2)}) %copy-start.1) | copy-done | bytes 524312
  2.8 0.0 copy-start.2
  2.8 1.0 %copy-done.2 = bf16[1,64,3072]{2,1,0:T(8,128)(2,1)S(1)} copy-done((bf16[1,64,3072]{2,1,0:T(8,128)(2,1)S(1)}, bf16[1,64,3072]{2,1,0:T(8,128)(2,1)}, u32[]{:S(2)}) %copy-start.2) | copy-done | bytes 393240
  3.8 0.0 copy-start.3
  3.8 0.9 %copy-done.3 = f32[256,128]{1,0:T(8,128)S(1)} copy-done((f32[256,128]{1,0:T(8,128)S(1)}, f32[256,128]{1,0:T(8,128)}, u32[]{:S(2)}) %copy-start.3) | copy-done | bytes 131096
  4.7 0.0 copy-start.4
  4.7 0.9 %copy-done.4 = f32[256,128]{1,0:T(8,128)S(1)} copy-done((f32[256,128]{1,0:T(8,128)S(1)}, f32[256,128]{1,0:T(8,128)}, u32[]{:S(2)}) %copy-start.4) | copy-done | bytes 131096
  5.6 0.0 copy-start.5
  5.6 0.7 %copy-done.5 = f32[1,3072]{1,0:T(1,128)S(1)} copy-done((f32[1,3072]{1,0:T(1,128)S(1)}, f32[1,3072]{1,0:T(1,128)}, u32[]{:S(2)}) %copy-start.5) | copy-done | bytes 12312
  6.3 0.0 copy-start.7
  6.3 0.0 copy-start.8
  6.3 38.0 %shard_map.162 = (bf16[128,3072]{1,0:T(8,128)(2,1)S(1)}, bf16[256,3072]{1,0:T(8,128)(2,1)}, bf16[256,2048]{1,0:T(8,128)(2,1)S(1)}, bf16[128,3072]{1,0:T(8,128)(2...) custom-call(bf16[128,3072]{1,0:T(8,128)(2,1)S(1)} %bitcast.10, ...), custom_call_target="tpu_custom_call" | custom-call | tf_op jit(solution)/shard_map/pallas_call | solution.py:629
  44.3 1.3 %collective-permute-start = (bf16[128,3072]{1,0:T(8,128)(2,1)S(1)}, bf16[128,3072]{1,0:T(8,128)(2,1)S(1)}, u32[]{:S(2)}, u32[]{:S(2)}) collective-permute-start(bf16[128,3072]{1,0:T(8,128)(2,1)S(1)} %get-tuple-element.29), channel_id=1, source_target_pairs={{0,1},{1,0},{2,3},{3,2},{4,5},{5,4},{6,7},{7,6},{8,9},{9,8},{10,11... | collective-permute-start | bytes 2359304 | tf_op jit(solution)/shard_map/ppermute | solution.py:682
  45.6 0.2 collective-permute-start.1
  45.9 0.0 copy-done.7
  45.9 0.0 copy-done.8
  45.9 0.0 copy-start.6
  45.9 1.4 %copy-done.6 = bf16[256,3072]{1,0:T(8,128)(2,1)S(1)} copy-done((bf16[256,3072]{1,0:T(8,128)(2,1)S(1)}, bf16[256,3072]{1,0:T(8,128)(2,1)}, u32[]{:S(2)}) %copy-start.6) | copy-done | bytes 1572888
  47.3 9.0 %shard_map.163 = (bf16[3072,1024]{1,0:T(8,128)(2,1)}, bf16[3072,512]{1,0:T(8,128)(2,1)}, bf16[3072,512]{1,0:T(8,128)(2,1)}, f32[64,3072]{1,0:T(8,128)}, f32[64,3072]{1,0:T(8,128)}) custom-call(bf16[256,3072]{1,0:T(8,128)(2,1)S(1)} %copy-done.6, bf16[256,2048]{1,0:T(8,128)(2,1)S(1)} %get-tuple-element.22.d_ref, ...), custom_call_target="tpu_custom_call" | custom-call | flops 3221225472 | bytes 18874368 | tf_op jit(solution)/shard_map/pallas_call | solution.py:686
  56.2 0.3 collective-permute-done.1.gain_b_ref
  56.5 0.0 collective-permute-done.landed_ref
  56.5 2.8 %shard_map.164 = (bf16[128,3072]{1,0:T(8,128)(2,1)}, f32[1,3072]{1,0:T(1,128)}) custom-call(bf16[128,3072]{1,0:T(8,128)(2,1)S(1)} %get-tuple-element.27.x_ref, bf16[128,3072]{1,0:T(8,128)(2,1)S(1)} %get-tuple-element.28.here_ref, f32[1,3072]{1,0:T(1,128)S(1)} %copy-done.5, bf16[128,3072]{1,0:T(8,128)(2,1)S(1)} %collective-permute-done.landed_ref, ...), custom_call_target="tpu_custom_call" | custom-call | flops 4718592 | bytes 1572864 | tf_op jit(solution)/shard_map/pallas_call | solution.py:711
Async XLA Ops:
  0.6 1.1 %copy-start = (bf16[1,128,3072]{2,1,0:T(8,128)(2,1)S(1)}, bf16[1,128,3072]{2,1,0:T(8,128)(2,1)}, u32[]{:S(2)}) copy-start(bf16[1,128,3072]{2,1,0:T(8,128)(2,1)} %param.11) | copy-start | bytes 2359300
  1.8 1.0 %copy-start.1 = (bf16[1,256,1024]{2,1,0:T(8,128)(2,1)S(1)}, bf16[1,256,1024]{2,1,0:T(8,128)(2,1)}, u32[]{:S(2)}) copy-start(bf16[1,256,1024]{2,1,0:T(8,128)(2,1)} %param.16) | copy-start | bytes 1572868
  2.8 1.0 %copy-start.2 = (bf16[1,64,3072]{2,1,0:T(8,128)(2,1)S(1)}, bf16[1,64,3072]{2,1,0:T(8,128)(2,1)}, u32[]{:S(2)}) copy-start(bf16[1,64,3072]{2,1,0:T(8,128)(2,1)} %param.19) | copy-start | bytes 1179652
  3.8 0.9 %copy-start.3 = (f32[256,128]{1,0:T(8,128)S(1)}, f32[256,128]{1,0:T(8,128)}, u32[]{:S(2)}) copy-start(f32[256,128]{1,0:T(8,128)} %constant.5.clone.sin_hbm) | copy-start | bytes 393220
  4.7 0.9 %copy-start.4 = (f32[256,128]{1,0:T(8,128)S(1)}, f32[256,128]{1,0:T(8,128)}, u32[]{:S(2)}) copy-start(f32[256,128]{1,0:T(8,128)} %constant.4.clone.cos_hbm) | copy-start | bytes 393220
  5.6 0.7 %copy-start.5 = (f32[1,3072]{1,0:T(1,128)S(1)}, f32[1,3072]{1,0:T(1,128)}, u32[]{:S(2)}) copy-start(f32[1,3072]{1,0:T(1,128)} %gain_ref.1) | copy-start | bytes 36868
  6.3 39.5 %copy-start.7 = (f32[64,3072]{1,0:T(8,128)S(1)}, f32[64,3072]{1,0:T(8,128)}, u32[]{:S(2)}) copy-start(f32[64,3072]{1,0:T(8,128)} %global_ref.1) | copy-start | bytes 2359300
  6.3 39.5 %copy-start.8 = (f32[64,3072]{1,0:T(8,128)S(1)}, f32[64,3072]{1,0:T(8,128)}, u32[]{:S(2)}) copy-start(f32[64,3072]{1,0:T(8,128)} %momentum_ref.1) | copy-start | bytes 2359300
  44.3 12.2 %collective-permute-start = (bf16[128,3072]{1,0:T(8,128)(2,1)S(1)}, bf16[128,3072]{1,0:T(8,128)(2,1)S(1)}, u32[]{:S(2)}, u32[]{:S(2)}) collective-permute-start(bf16[128,3072]{1,0:T(8,128)(2,1)S(1)} %get-tuple-element.29), channel_id=1, source_target_pairs={{0,1},{1,0},{2,3},{3,2},{4,5},{5,4},{6,7},{7,6},{8,9},{9,8},{10,11... | collective-permute-start | bytes 2359304 | tf_op jit(solution)/shard_map/ppermute | solution.py:682
  45.6 10.9 %collective-permute-start.1 = (f32[1,3072]{1,0:T(1,128)S(1)}, f32[1,3072]{1,0:T(1,128)S(1)}, u32[]{:S(2)}, u32[]{:S(2)}) collective-permute-start(f32[1,3072]{1,0:T(1,128)S(1)} %get-tuple-element.30.gain_a_ref), channel_id=1, source_target_pairs={{0,1},{1,0},{2,3},{3,2},{4,5},{5,4},{6,7},{7,6},{8,9},{9,8},{10,11... | collective-permute-start | bytes 36872 | tf_op jit(solution)/shard_map/ppermute | solution.py:683
  45.9 1.4 %copy-start.6 = (bf16[256,3072]{1,0:T(8,128)(2,1)S(1)}, bf16[256,3072]{1,0:T(8,128)(2,1)}, u32[]{:S(2)}) copy-start(bf16[256,3072]{1,0:T(8,128)(2,1)} %get-tuple-element.21.nm_ref) | copy-start | bytes 4718596

commit v2 on v1

--- a/solution.py
+++ b/solution.py
@@ -245,7 +245,7 @@
     nm_ref,
     d_ref,
     here_ref,
-    far_hbm,
+    far_ref,
     gain_part_ref,
     mean_ref,
     gain_ref,
@@ -257,12 +257,10 @@
     q_ref,
     k_ref,
     v_ref,
-    far_ref,
     pieces_ref,
     own_mean_ref,
     in_sems,
     w_sems,
-    far_sems,
     ag_send,
     ag_recv,
     fr_send,
@@ -529,33 +527,32 @@
 
     lax.fori_loop(0, heads_kv, kv_head, 0)
 
-    def far_copy(t):
-        return pltpu.make_async_copy(
-            far_ref.at[:, ds(t, tile)], far_hbm.at[:, ds(t, tile)], far_sems.at[t]
-        )
-
     def back(t, _):
         both = jnp.concatenate([d_ref[ds(peer, rows), :], d_ref[ds(me, rows), :]], axis=0)
         part = dot(both, w_ref[ds(t, tile), :], NT).astype(jnp.bfloat16)
         cols = ds(t, tile)
-        far_ref[:, cols] = part[:rows]
+        far_ref[pl.ds(0, rows), cols] = part[:rows]
         here_ref[:, cols] = part[rows:]
         wide = part.astype(jnp.float32)
         products = wide[:rows] * nm_ref[ds(peer, rows), cols].astype(jnp.float32)
         products += wide[rows:] * nm_ref[ds(me, rows), cols].astype(jnp.float32)
-        gain_part_ref[:, cols] = jnp.sum(products, axis=0, keepdims=True) / gain_ref[:, cols]
-        far_copy(t).start()
+        gain_part = jnp.sum(products, axis=0, keepdims=True) / gain_ref[:, cols]
+        gain_part_ref[:, cols] = gain_part
+        lines = []
+        for _ in range(3):
+            lines.append(gain_part.astype(jnp.bfloat16).astype(jnp.float32))
+            gain_part = gain_part - lines[-1]
+        lines = jnp.concatenate(lines + [jnp.zeros((pad - 3, tile), jnp.float32)], axis=0)
+        far_ref[pl.ds(rows, pad), cols] = lines.astype(jnp.bfloat16)
         return 0
 
-    tiles = width // tile
-    lax.fori_loop(0, tiles, back, 0)
+    pad = far_ref.shape[0] - rows
+    lax.fori_loop(0, width // tile, back, 0)
 
     wait_recv_all(lambda j: spread_copy(j, lax.rem(rep + n_rep - j, n_rep)), 1, n_rep)
     wait_send_all(gather_copy, 0, chunks)
     wait_send_all(scatter_copy, 1, n_rep)
     wait_send_all(lambda j: spread_copy(j, rep), 1, n_rep)
-    for t in range(tiles):
-        far_copy(t).wait()
 
 
 def weights_kernel(nm_ref, d_ref, mean_ref, global_ref, momentum_ref, gq_ref, gk_ref, gv_ref, ng_ref, nmom_ref):
@@ -573,31 +570,30 @@
     ng_ref[...] = held - outer_rate * (mean_delta + outer_momentum * new_momentum)
 
 
-def rows_kernel(x_ref, here_ref, gain_ref, landed_ref, gain_a_ref, gain_b_ref, out_ref, gain_out_ref):
+def rows_kernel(x_ref, here_ref, gain_ref, landed_ref, gain_part_ref, out_ref, gain_out_ref):
     i = pl.program_id(0)
-    count = landed_ref.shape[0]
+    count = out_ref.shape[0]
+    rows, width = x_ref.shape
 
     @pl.when(i == 0)
     def _():
-        gain_out_ref[...] = gain_a_ref[...] + gain_b_ref[...]
+        lines = landed_ref[pl.ds(rows, landed_ref.shape[0] - rows), :].astype(jnp.float32)
+        gain_out_ref[...] = gain_part_ref[...] + (lines[2:3] + lines[1:2] + lines[:1])
 
     step = 16
 
     def some(j, _):
         block = pl.ds(pl.multiple_of(i * count + j * step, step), step)
-        part = ds(j, step)
         x = x_ref[block, :].astype(jnp.float32)
         inverse = lax.rsqrt(jnp.mean(x * x, axis=-1, keepdims=True) + epsilon)
-        xhat = x * inverse
         scaled = (
-            here_ref[block, :].astype(jnp.float32) + landed_ref[part, :].astype(jnp.float32)
+            here_ref[block, :].astype(jnp.float32) + landed_ref[block, :].astype(jnp.float32)
         ) * gain_ref[...]
-        out_ref[part, :] = (
-            inverse * (scaled - xhat * jnp.mean(scaled * xhat, axis=-1, keepdims=True))
-        ).astype(jnp.bfloat16)
+        pull = jnp.mean(scaled * x, axis=-1, keepdims=True) * (inverse * inverse)
+        out_ref[ds(j, step), :] = (inverse * (scaled - x * pull)).astype(jnp.bfloat16)
         return 0
 
-    lax.fori_loop(0, count // step, some, 0)
+    lax.fori_loop(0, count // step, some, 0, unroll=2)
 
 
 def pair_body(
@@ -622,6 +618,7 @@
     piece_cols = width * frag_rows // piece_rows // n_rep
     chunks = 6
     tile = 512
+    pad = 8
     bf16, f32 = jnp.bfloat16, jnp.float32
     cosine, sine = host_tables(sequence, HEAD_SIZE)
     vmem = pl.BlockSpec(memory_space=pltpu.VMEM)
@@ -629,16 +626,16 @@
     x, normed, d, here, far, gain_partial, mean_local = pl.pallas_call(
         functools.partial(front_kernel, n_rep, chunks, tile),
         out_shape=(
-            jax.ShapeDtypeStruct((rows, width), bf16),
-            jax.ShapeDtypeStruct((sequence, width), bf16),
-            jax.ShapeDtypeStruct((sequence, total), bf16),
-            jax.ShapeDtypeStruct((rows, width), bf16),
-            jax.ShapeDtypeStruct((rows, width), bf16),
-            jax.ShapeDtypeStruct((1, width), f32),
-            jax.ShapeDtypeStruct((frag_rows, width), bf16),
+            pltpu.VMEM((rows, width), bf16),
+            pltpu.VMEM((sequence, width), bf16),
+            pltpu.VMEM((sequence, total), bf16),
+            pltpu.VMEM((rows, width), bf16),
+            pltpu.VMEM((rows + pad, width), bf16),
+            pltpu.VMEM((1, width), f32),
+            pltpu.VMEM((frag_rows, width), bf16),
         ),
         in_specs=[hbm] * 9,
-        out_specs=(vmem, vmem, vmem, vmem, hbm, vmem, vmem),
+        out_specs=(vmem,) * 7,
         scratch_shapes=[
             pltpu.VMEM((1, width), f32),
             pltpu.VMEM((sequence, qw), bf16),
@@ -649,12 +646,10 @@
             pltpu.VMEM((sequence, qw), bf16),
             pltpu.VMEM((sequence, kw), bf16),
             pltpu.VMEM((sequence, kw), bf16),
-            pltpu.VMEM((rows, width), bf16),
             pltpu.VMEM((n_rep, piece_rows, piece_cols), bf16),
             pltpu.VMEM((piece_rows, piece_cols), bf16),
             pltpu.SemaphoreType.DMA((5,)),
             pltpu.SemaphoreType.DMA((total // tile,)),
-            pltpu.SemaphoreType.DMA((width // tile,)),
             pltpu.SemaphoreType.DMA((chunks,)),
             pltpu.SemaphoreType.DMA((chunks,)),
             pltpu.SemaphoreType.DMA((n_rep,)),
@@ -668,19 +663,23 @@
             collective_id=0, has_side_effects=True, vmem_limit_bytes=48 * 1024 * 1024
         ),
     )(
-        tokens[0],
-        norm_gain,
-        weight_q,
-        weight_k,
-        weight_v,
-        attention_gradient[0],
-        cosine,
-        sine,
-        local_fragment[0],
+        *[
+            pltpu.with_memory_space_constraint(array, pltpu.HBM)
+            for array in (
+                tokens[0],
+                norm_gain,
+                weight_q,
+                weight_k,
+                weight_v,
+                attention_gradient[0],
+                cosine,
+                sine,
+                local_fragment[0],
+            )
+        ]
     )
     swap = [(0, 1), (1, 0)]
     landed = lax.ppermute(far, "tp", swap)
-    gain_landed = lax.ppermute(gain_partial, "tp", swap)
     wide = 256
     columns = lambda size: pl.BlockSpec((size, wide), lambda i: (0, i))
     grad_wq, grad_wk, grad_wv, new_global, new_momentum = pl.pallas_call(
@@ -715,13 +714,13 @@
             jax.ShapeDtypeStruct((rows, width), bf16),
             jax.ShapeDtypeStruct((1, width), f32),
         ),
-        in_specs=[vmem, vmem, vmem, block, vmem, vmem],
+        in_specs=[vmem] * 5,
         out_specs=(block, pl.BlockSpec((1, width), lambda i: (0, 0))),
         compiler_params=pltpu.CompilerParams(vmem_limit_bytes=8 * 1024 * 1024),
         cost_estimate=pl.CostEstimate(
             flops=12 * rows * width, bytes_accessed=4 * rows * width, transcendentals=0
         ),
-    )(x, here, norm_gain, landed, gain_partial, gain_landed)
+    )(x, here, norm_gain, landed, gain_partial)
     return (
         grad_wq[None],
         grad_wk[None],

time: 59.7 us -> 52.6 us (0.88)
  local copies, waits for them, and re-layouts: 7.09 us -> 0.01 us
  waiting for transfers between devices: 0.31 us -> 2.71 us
  Pallas kernels: 49.8 us -> 47.8 us
    unnamed x18 -> x6, local copies, waits for them, and re-layouts: 7.09 us -> 0.01 us
    ppermute x1, waiting for transfers between devices: 0.01 us -> 2.71 us  [pair_body(): landed = lax.ppermute(far, 'tp', swap)]
    pallas_call x1, Pallas kernels: 38 us -> 36.7 us  [pair_body(): pl.pallas_call(functools.partial(front_kernel, n_rep, chunks, tile), out_...]
    pallas_call x1, Pallas kernels: 2.83 us -> 2.06 us  [pair_body(): pl.pallas_call(rows_kernel, grid=(rows // count,), out_shape=(jax.ShapeDt...]
  transfers between devices with their start and end apart: 2 -> 1, of which waited for: 1 -> 1; matrix products, arithmetic and copies ran while one was open for 0% -> 0% of each run, Pallas kernels for 15% -> 17%
where the time goes in v2:
time: 52.6 us; the launch traced here: 52.5 us
  Pallas kernels  47.8 us (91%)
  waiting for transfers between devices  2.71 us (5%)
  starting transfers between devices  1.31 us (2%)
  between operations  0.66 us (1%)
    pallas_call x1, Pallas kernels, pair_body(): pl.pallas_call(functools.partial(front_kernel, n_rep, chunks, tile), out_...  36.7 us
    pallas_call x1, Pallas kernels, pair_body(): pl.pallas_call(weights_kernel, grid=(width // wide,), out_shape=(jax.Shap...  8.97 us
    ppermute x1, waiting for transfers between devices, pair_body(): landed = lax.ppermute(far, 'tp', swap)  2.71 us
    pallas_call x1, Pallas kernels, pair_body(): pl.pallas_call(rows_kernel, grid=(rows // count,), out_shape=(jax.ShapeDt...  2.06 us
    ppermute x1, starting transfers between devices, pair_body(): landed = lax.ppermute(far, 'tp', swap)  1.31 us
  transfers between devices with their start and end apart: 1, of which 1 were waited for; matrix products, arithmetic and copies ran while one was open for 0% of the time, Pallas kernels for 17%

profile of v2, /device:TPU:1, one launch (start us, length us, event | category | flops | bytes accessed | tf_op | source)
XLA Modules:
  0.0 52.5 jit_solution(9850552727947523480)
XLA Ops:
  0.6 0.0 copy-start.1
  0.6 0.0 copy-start.2
  0.7 36.7 %shard_map.162 = (bf16[128,3072]{1,0:T(8,128)(2,1)S(1)}, bf16[256,3072]{1,0:T(8,128)(2,1)S(1)}, bf16[256,2048]{1,0:T(8,128)(2,1)S(1)}, bf16[128,3072]{1,0:T(8,12...) custom-call(bf16[128,3072]{1,0:T(8,128)(2,1)} %bitcast.13, ...), custom_call_target="tpu_custom_call" | custom-call | tf_op jit(solution)/shard_map/pallas_call | solution.py:626
  37.4 1.3 %collective-permute-start = (bf16[136,3072]{1,0:T(8,128)(2,1)S(1)}, bf16[136,3072]{1,0:T(8,128)(2,1)S(1)}, u32[]{:S(2)}, u32[]{:S(2)}) collective-permute-start(bf16[136,3072]{1,0:T(8,128)(2,1)S(1)} %get-tuple-element.29), channel_id=1, source_target_pairs={{0,1},{1,0},{2,3},{3,2},{4,5},{5,4},{6,7},{7,6},{8,9},{9,8},{10,11... | collective-permute-start | bytes 2506760 | tf_op jit(solution)/shard_map/ppermute | solution.py:682
  38.7 0.0 copy-done.1
  38.7 0.0 copy-done.2
  38.7 0.0 copy-start
  38.7 9.0 %shard_map.163 = (bf16[3072,1024]{1,0:T(8,128)(2,1)}, bf16[3072,512]{1,0:T(8,128)(2,1)}, bf16[3072,512]{1,0:T(8,128)(2,1)}, f32[64,3072]{1,0:T(8,128)}, f32[64,3072]{1,0:T(8,128)}) custom-call(bf16[256,3072]{1,0:T(8,128)(2,1)S(1)} %get-tuple-element.21.nm_ref, bf16[256,2048]{1,0:T(8,128)(2,1)S(1)} %get-tuple-element.22.d_ref, ...), custom_call_target="tpu_custom_call" | custom-call | flops 3221225472 | bytes 18874368 | tf_op jit(solution)/shard_map/pallas_call | solution.py:685
  47.7 2.7 %collective-permute-done.landed_ref = bf16[136,3072]{1,0:T(8,128)(2,1)S(1)} collective-permute-done((bf16[136,3072]{1,0:T(8,128)(2,1)S(1)}, bf16[136,3072]{1,0:T(8,128)(2,1)S(1)}, u32[]{:S(2)}, u32[]{:S(2)}) %collective-permute-start) | collective-permute-done | bytes 835616 | tf_op jit(solution)/shard_map/ppermute | solution.py:682
  50.4 0.0 copy-done
  50.4 2.1 %shard_map.164 = (bf16[128,3072]{1,0:T(8,128)(2,1)}, f32[1,3072]{1,0:T(1,128)}) custom-call(bf16[128,3072]{1,0:T(8,128)(2,1)S(1)} %get-tuple-element.27.x_ref, bf16[128,3072]{1,0:T(8,128)(2,1)S(1)} %get-tuple-element.28.here_ref, f32[1,3072]{1,0:T(1,128)S(1)} %copy-done, bf16[136,3072]{1,0:T(8,128)(2,1)S(1)} %collective-permute-done.landed_ref, ...), custom_call_target="tpu_custom_call" | custom-call | flops 4718592 | bytes 1572864 | tf_op jit(solution)/shard_map/pallas_call | solution.py:710
Async XLA Ops:
  0.6 38.1 %copy-start.1 = (f32[64,3072]{1,0:T(8,128)S(1)}, f32[64,3072]{1,0:T(8,128)}, u32[]{:S(2)}) copy-start(f32[64,3072]{1,0:T(8,128)} %global_ref.1) | copy-start | bytes 2359300
  0.6 38.1 %copy-start.2 = (f32[64,3072]{1,0:T(8,128)S(1)}, f32[64,3072]{1,0:T(8,128)}, u32[]{:S(2)}) copy-start(f32[64,3072]{1,0:T(8,128)} %momentum_ref.1) | copy-start | bytes 2359300
  37.4 13.0 %collective-permute-start = (bf16[136,3072]{1,0:T(8,128)(2,1)S(1)}, bf16[136,3072]{1,0:T(8,128)(2,1)S(1)}, u32[]{:S(2)}, u32[]{:S(2)}) collective-permute-start(bf16[136,3072]{1,0:T(8,128)(2,1)S(1)} %get-tuple-element.29), channel_id=1, source_target_pairs={{0,1},{1,0},{2,3},{3,2},{4,5},{5,4},{6,7},{7,6},{8,9},{9,8},{10,11... | collective-permute-start | bytes 2506760 | tf_op jit(solution)/shard_map/ppermute | solution.py:682
  38.7 11.7 %copy-start = (f32[1,3072]{1,0:T(1,128)S(1)}, f32[1,3072]{1,0:T(1,128)}, u32[]{:S(2)}) copy-start(f32[1,3072]{1,0:T(1,128)} %gain_ref.1) | copy-start | bytes 36868

commit v3 on v2

--- a/solution.py
+++ b/solution.py
@@ -8,6 +8,7 @@
 from jax.experimental.pallas import tpu as pltpu
 from jax.sharding import PartitionSpec as P
 
+
 MESH = pl.DeviceIdType.MESH
 
 HEAD_SIZE = 128
@@ -18,6 +19,8 @@
 outer_rate = 0.7
 outer_momentum = 0.9
 LOG2_E = 1.4426950408889634
+LANES = 128
+SUBLANES = 8
 
 
 def rope_tables(sequence_length, width):
@@ -205,6 +208,7 @@
         new_momentum,
     )
 
+
 NT = (((1,), (1,)), ((), ()))
 TN = (((0,), (0,)), ((), ()))
 
@@ -226,6 +230,29 @@
         jnp.asarray(np.concatenate([cosine, cosine], axis=1), jnp.float32),
         jnp.asarray(np.concatenate([-sine, sine], axis=1), jnp.float32),
     )
+
+
+def shares(d_ref, nm_ref, w_ref, gain_ref, far_ref, here_ref, gain_part_ref, low, tile):
+    me = lax.axis_index("tp")
+    peer = 1 - me
+    rows = here_ref.shape[0]
+    offset = gain_part_ref.shape[1] - here_ref.shape[1] if low else 0
+
+    def back(t, _):
+        both = jnp.concatenate([d_ref[ds(peer, rows), :], d_ref[ds(me, rows), :]], axis=0)
+        cols = pl.ds(pl.multiple_of(low + t * tile, tile), tile)
+        own = ds(t, tile)
+        part = dot(both, w_ref[cols, :], NT).astype(jnp.bfloat16)
+        far_ref[pl.ds(0, rows), own] = part[:rows]
+        here_ref[:, own] = part[rows:]
+        wide = part.astype(jnp.float32)
+        products = wide[:rows] * nm_ref[ds(peer, rows), cols].astype(jnp.float32)
+        products += wide[rows:] * nm_ref[ds(me, rows), cols].astype(jnp.float32)
+        gain_part = jnp.sum(products, axis=0, keepdims=True) / gain_ref[:, cols]
+        gain_part_ref[:, pl.ds(pl.multiple_of(offset + t * tile, tile), tile)] = gain_part
+        return 0
+
+    lax.fori_loop(0, here_ref.shape[1] // tile, back, 0)
 
 
 def front_kernel(
@@ -248,15 +275,21 @@
     far_ref,
     gain_part_ref,
     mean_ref,
+    w_ref,
     gain_ref,
     go_ref,
     cos_ref,
     sin_ref,
-    w_ref,
     acc_ref,
     q_ref,
     k_ref,
     v_ref,
+    raw_ref,
+    wide_ref,
+    inv_ref,
+    mine_ref,
+    theirs_ref,
+    pair_ref,
     pieces_ref,
     own_mean_ref,
     in_sems,
@@ -267,6 +300,7 @@
     fr_recv,
     fg_send,
     fg_recv,
+    pair_sems,
     own_sem,
     go_sem,
 ):
@@ -274,22 +308,31 @@
     peer = 1 - me
     rep = lax.axis_index("rep")
     side = lax.rem(rep, 2)
+    partner = rep + 1 - 2 * side
+    lane = rep // 2
+    n_lanes = n_rep // 2
     rows, width = x_ref.shape
     qw, kw = wq_hbm.shape[1], wk_hbm.shape[1]
     total = qw + 2 * kw
     cw = width // chunks
     piece_rows, piece_cols = own_mean_ref.shape
     col_blocks = width // piece_cols
+
+    def along(j):
+        return 2 * lax.rem(lane + j, n_lanes) + side
+
     barrier = pltpu.get_barrier_semaphore()
     pl.semaphore_signal(barrier, inc=1, device_id={"tp": peer}, device_id_type=MESH)
-
-    def greet(j, _):
-        pl.semaphore_signal(
-            barrier, inc=1, device_id={"rep": lax.rem(rep + j, n_rep)}, device_id_type=MESH
-        )
-        return 0
-
-    lax.fori_loop(1, n_rep, greet, 0)
+    pl.semaphore_signal(barrier, inc=1, device_id={"rep": partner}, device_id_type=MESH)
+
+    @pl.when(side == 1)
+    def _():
+        def greet(j, _):
+            pl.semaphore_signal(barrier, inc=1, device_id={"rep": along(j)}, device_id_type=MESH)
+            return 0
+
+        lax.fori_loop(1, n_lanes, greet, 0)
+
     first_copies = [
         pltpu.make_async_copy(tokens_hbm, x_ref, in_sems.at[0]),
         pltpu.make_async_copy(gain_hbm, gain_ref, in_sems.at[1]),
@@ -299,6 +342,7 @@
         pltpu.make_async_copy(sin_hbm, sin_ref, in_sems.at[3]),
         pltpu.make_async_copy(go_hbm, go_ref, in_sems.at[4]),
     ]
+    half_copy = pltpu.make_async_copy(local_hbm, mine_ref, own_sem)
     weight_copies = []
     for source, offset in ((wq_hbm, 0), (wk_hbm, qw), (wv_hbm, qw + kw)):
         for t in range(source.shape[1] // tile):
@@ -309,6 +353,49 @@
                     w_sems.at[len(weight_copies)],
                 )
             )
+    for copy in first_copies:
+        copy.start()
+
+    @pl.when(side == 1)
+    def _():
+        half_copy.start()
+
+
+    def gather_copy(c):
+        return pltpu.make_async_remote_copy(
+            src_ref=tokens_hbm.at[:, ds(c, cw)],
+            dst_ref=raw_ref.at[:, ds(c, cw)],
+            send_sem=ag_send.at[c],
+            recv_sem=ag_recv.at[c],
+            device_id={"tp": peer},
+            device_id_type=MESH,
+        )
+
+    norm_copy = pltpu.make_async_remote_copy(
+        src_ref=inv_ref.at[0],
+        dst_ref=inv_ref.at[1],
+        send_sem=pair_sems.at[0],
+        recv_sem=pair_sems.at[1],
+        device_id={"tp": peer},
+        device_id_type=MESH,
+    )
+    pair_copy = pltpu.make_async_remote_copy(
+        src_ref=local_hbm,
+        dst_ref=theirs_ref,
+        send_sem=pair_sems.at[2],
+        recv_sem=pair_sems.at[3],
+        device_id={"rep": partner},
+        device_id_type=MESH,
+    )
+
+    mean_copy = pltpu.make_async_remote_copy(
+        src_ref=mean_ref,
+        dst_ref=mean_ref,
+        send_sem=pair_sems.at[4],
+        recv_sem=pair_sems.at[5],
+        device_id={"rep": partner},
+        device_id_type=MESH,
+    )
 
     def piece(owner):
         return (
@@ -316,46 +403,13 @@
             ds(lax.rem(owner, col_blocks), piece_cols),
         )
 
-    own_piece = pltpu.make_async_copy(local_hbm.at[piece(rep)], pieces_ref.at[0], own_sem)
-    for copy in first_copies + weight_copies[:1] + late_copies[:2] + weight_copies[1:]:
-        copy.start()
-    own_piece.start()
-    late_copies[2].start()
-    for copy in first_copies:
-        copy.wait()
-
-    step = 16
-
-    def norm_rows(i, _):
-        x = x_ref[ds(i, step), :].astype(jnp.float32)
-        inverse = lax.rsqrt(jnp.mean(x * x, axis=-1, keepdims=True) + epsilon)
-        nm_ref[pl.ds(pl.multiple_of(me * rows + i * step, step), step), :] = (
-            x * inverse * gain_ref[...]
-        ).astype(jnp.bfloat16)
-        return 0
-
-    lax.fori_loop(0, rows // step, norm_rows, 0)
-    pl.semaphore_wait(barrier, n_rep)
-
-    def gather_copy(c):
-        part = nm_ref.at[ds(me, rows), ds(c, cw)]
+    def scatter_copy(j):
         return pltpu.make_async_remote_copy(
-            src_ref=part,
-            dst_ref=part,
-            send_sem=ag_send.at[c],
-            recv_sem=ag_recv.at[c],
-            device_id={"tp": peer},
-            device_id_type=MESH,
-        )
-
-    def scatter_copy(j):
-        target = lax.rem(rep + j, n_rep)
-        return pltpu.make_async_remote_copy(
-            src_ref=local_hbm.at[piece(target)],
+            src_ref=pair_ref.at[piece(lax.rem(lane + j, n_lanes))],
             dst_ref=pieces_ref.at[j],
             send_sem=fr_send.at[j],
             recv_sem=fr_recv.at[j],
-            device_id={"rep": target},
+            device_id={"rep": along(j)},
             device_id_type=MESH,
         )
 
@@ -365,7 +419,7 @@
             dst_ref=mean_ref.at[piece(owner)],
             send_sem=fg_send.at[j],
             recv_sem=fg_recv.at[j],
-            device_id={"rep": lax.rem(rep + j, n_rep)},
+            device_id={"rep": along(j)},
             device_id_type=MESH,
         )
 
@@ -390,12 +444,48 @@
 
         lax.fori_loop(low, high, one, 0)
 
+    early = chunks // 3
+    pl.semaphore_wait(barrier, 2 + side * (n_lanes - 1))
+
     @pl.when(side == 0)
     def _():
-        start_all(gather_copy, 0, chunks)
-
-    start_all(scatter_copy, 1, n_rep)
-
+        start_all(gather_copy, 0, early)
+        pair_copy.start()
+
+    for copy in first_copies:
+        copy.wait()
+    for copy in weight_copies + late_copies:
+        copy.start()
+
+    step = 16
+
+    def norm_rows(i, _):
+        x = x_ref[ds(i, step), :].astype(jnp.float32)
+        inverse = lax.rsqrt(jnp.mean(x * x, axis=-1, keepdims=True) + epsilon)
+        wide_ref[ds(i, step), :] = jnp.broadcast_to(inverse, (step, LANES))
+        nm_ref[pl.ds(pl.multiple_of(me * rows + i * step, step), step), :] = (
+            x * inverse * gain_ref[...]
+        ).astype(jnp.bfloat16)
+        return 0
+
+    lax.fori_loop(0, rows // step, norm_rows, 0)
+    inv_ref[0] = wide_ref[...].T[:SUBLANES]
+    norm_copy.start()
+
+    @pl.when(side == 0)
+    def _():
+        start_all(gather_copy, early, chunks)
+
+    @pl.when(side == 1)
+    def _():
+        half_copy.wait()
+        pair_copy.wait_recv()
+        pair_ref[...] = (
+            mine_ref[...].astype(jnp.float32) + theirs_ref[...].astype(jnp.float32)
+        ).astype(jnp.bfloat16)
+        start_all(scatter_copy, 1, n_lanes)
+
+    heads_q, heads_kv = qw // HEAD_SIZE, kw // HEAD_SIZE
     for t, copy in enumerate(weight_copies):
         copy.wait()
         acc_ref[ds(me, rows), pl.ds(t * tile, tile)] = dot(
@@ -404,8 +494,6 @@
     acc_ref[ds(peer, rows), :] = jnp.zeros((rows, total), jnp.float32)
     for copy in late_copies:
         copy.wait()
-
-    heads_q, heads_kv = qw // HEAD_SIZE, kw // HEAD_SIZE
 
     def rope_rows(which):
         block = ds(which, rows)
@@ -426,45 +514,53 @@
     rope_rows(me)
 
     def average_pieces():
-        own_piece.wait()
-        wait_recv_all(scatter_copy, 1, n_rep)
-        summed = pieces_ref[0].astype(jnp.float32)
-        for j in range(1, n_rep):
+        wait_recv_all(scatter_copy, 1, n_lanes)
+        summed = pair_ref[piece(lane)].astype(jnp.float32)
+        for j in range(1, n_lanes):
             summed = summed + pieces_ref[j].astype(jnp.float32)
         summed = (summed * (1.0 / n_rep)).astype(jnp.bfloat16)
         own_mean_ref[...] = summed
-        mean_ref[piece(rep)] = summed
-        start_all(lambda j: spread_copy(j, rep), 1, n_rep)
+        mean_ref[piece(lane)] = summed
+        start_all(lambda j: spread_copy(j, lane), 1, n_lanes)
+
+    def pass_mean():
+        wait_recv_all(
+            lambda j: spread_copy(j, lax.rem(lane + n_lanes - j, n_lanes)), 1, n_lanes
+        )
+        mean_copy.start()
 
     @pl.when(side == 1)
     def _():
+        average_pieces()
         pl.semaphore_wait(go_sem, 1)
         start_all(gather_copy, 0, chunks)
-        average_pieces()
+
+    norm_copy.wait_recv()
+    wide_ref[...] = jnp.broadcast_to(inv_ref[1][:1], (LANES, rows)).T
 
     def arrived(c, _):
-        pltpu.make_async_remote_copy(
-            src_ref=nm_ref.at[ds(peer, rows), ds(c, cw)],
-            dst_ref=nm_ref.at[ds(peer, rows), ds(c, cw)],
-            send_sem=ag_send.at[c],
-            recv_sem=ag_recv.at[c],
-            device_id={"tp": peer},
-            device_id_type=MESH,
-        ).wait_recv()
-
-        @pl.when((side == 0) & (c == chunks - 2))
+        gather_copy(c).wait_recv()
+
+        @pl.when((side == 0) & (c == chunks - 4))
         def _():
-            pl.semaphore_signal(
-                go_sem, inc=1, device_id={"rep": lax.rem(rep + 1, n_rep)}, device_id_type=MESH
+            pl.semaphore_signal(go_sem, inc=1, device_id={"rep": partner}, device_id_type=MESH)
+
+        @pl.when((side == 1) & (c == chunks - 5))
+        def _():
+            pass_mean()
+
+        inverse = wide_ref[...]
+        parts = []
+        for part in range(cw // LANES):
+            cols = pl.ds(pl.multiple_of(c * cw + part * LANES, LANES), LANES)
+            parts.append(
+                (raw_ref[:, cols].astype(jnp.float32) * inverse * gain_ref[:, cols]).astype(
+                    jnp.bfloat16
+                )
             )
-
-        part = nm_ref[ds(peer, rows), ds(c, cw)]
-
-        def one(t, _):
-            acc_ref[ds(peer, rows), ds(t, tile)] += dot(part, w_ref[ds(c, cw), ds(t, tile)])
-            return 0
-
-        lax.fori_loop(0, total // tile, one, 0)
+        part = jnp.concatenate(parts, axis=1)
+        nm_ref[ds(peer, rows), ds(c, cw)] = part
+        acc_ref[ds(peer, rows), :] += dot(part, w_ref[ds(c, cw), :])
         return 0
 
     lax.fori_loop(0, chunks, arrived, 0)
@@ -483,10 +579,6 @@
         return (gradient * c - pltpu.roll(gradient, HEAD_SIZE // 2, 1) * s).astype(jnp.bfloat16)
 
     def kv_head(g, _):
-        @pl.when((side == 0) & (g == 1))
-        def _():
-            average_pieces()
-
         grad_k = [None, None]
         grad_v = [None, None]
         kv = ds(g, HEAD_SIZE)
@@ -525,34 +617,41 @@
             d_ref[block, ds(heads_q + heads_kv + g, HEAD_SIZE)] = grad_v[j].astype(jnp.bfloat16)
         return 0
 
-    lax.fori_loop(0, heads_kv, kv_head, 0)
-
-    def back(t, _):
-        both = jnp.concatenate([d_ref[ds(peer, rows), :], d_ref[ds(me, rows), :]], axis=0)
-        part = dot(both, w_ref[ds(t, tile), :], NT).astype(jnp.bfloat16)
-        cols = ds(t, tile)
-        far_ref[pl.ds(0, rows), cols] = part[:rows]
-        here_ref[:, cols] = part[rows:]
-        wide = part.astype(jnp.float32)
-        products = wide[:rows] * nm_ref[ds(peer, rows), cols].astype(jnp.float32)
-        products += wide[rows:] * nm_ref[ds(me, rows), cols].astype(jnp.float32)
-        gain_part = jnp.sum(products, axis=0, keepdims=True) / gain_ref[:, cols]
-        gain_part_ref[:, cols] = gain_part
-        lines = []
+    lax.fori_loop(0, heads_kv, kv_head, 0, unroll=True)
+
+    shares(d_ref, nm_ref, w_ref, gain_ref, far_ref, here_ref, gain_part_ref, 0, tile)
+
+    norm_copy.wait_send()
+    wait_send_all(gather_copy, 0, chunks)
+
+    @pl.when(side == 0)
+    def _():
+        pair_copy.wait_send()
+        mean_copy.wait_recv()
+
+    @pl.when(side == 1)
+    def _():
+        wait_send_all(scatter_copy, 1, n_lanes)
+        wait_send_all(lambda j: spread_copy(j, lane), 1, n_lanes)
+        mean_copy.wait_send()
+
+
+def second_kernel(
+    tile, d_ref, nm_ref, w_ref, gain_ref, gain_a_ref, far_ref, here_ref, gain_part_ref
+):
+    rows, cols = here_ref.shape
+    done = gain_a_ref.shape[1]
+    gain_part_ref[:, pl.ds(0, done)] = gain_a_ref[...]
+    shares(d_ref, nm_ref, w_ref, gain_ref, far_ref, here_ref, gain_part_ref, done, tile)
+    lines = []
+    for low in range(0, done + cols, cols):
+        gain_part = gain_part_ref[:, pl.ds(low, cols)]
         for _ in range(3):
             lines.append(gain_part.astype(jnp.bfloat16).astype(jnp.float32))
             gain_part = gain_part - lines[-1]
-        lines = jnp.concatenate(lines + [jnp.zeros((pad - 3, tile), jnp.float32)], axis=0)
-        far_ref[pl.ds(rows, pad), cols] = lines.astype(jnp.bfloat16)
-        return 0
-
     pad = far_ref.shape[0] - rows
-    lax.fori_loop(0, width // tile, back, 0)
-
-    wait_recv_all(lambda j: spread_copy(j, lax.rem(rep + n_rep - j, n_rep)), 1, n_rep)
-    wait_send_all(gather_copy, 0, chunks)
-    wait_send_all(scatter_copy, 1, n_rep)
-    wait_send_all(lambda j: spread_copy(j, rep), 1, n_rep)
+    lines = jnp.concatenate(lines + [jnp.zeros((pad - len(lines), cols), jnp.float32)], axis=0)
+    far_ref[pl.ds(rows, pad), :] = lines.astype(jnp.bfloat16)
 
 
 def weights_kernel(nm_ref, d_ref, mean_ref, global_ref, momentum_ref, gq_ref, gk_ref, gv_ref, ng_ref, nmom_ref):
@@ -570,15 +669,18 @@
     ng_ref[...] = held - outer_rate * (mean_delta + outer_momentum * new_momentum)
 
 
-def rows_kernel(x_ref, here_ref, gain_ref, landed_ref, gain_part_ref, out_ref, gain_out_ref):
+def rows_kernel(
+    x_ref, here_a_ref, here_b_ref, gain_ref, landed_a_ref, landed_b_ref, part_ref, out_ref, gain_out_ref
+):
     i = pl.program_id(0)
     count = out_ref.shape[0]
-    rows, width = x_ref.shape
+    rows, _ = x_ref.shape
 
     @pl.when(i == 0)
     def _():
-        lines = landed_ref[pl.ds(rows, landed_ref.shape[0] - rows), :].astype(jnp.float32)
-        gain_out_ref[...] = gain_part_ref[...] + (lines[2:3] + lines[1:2] + lines[:1])
+        lines = landed_b_ref[pl.ds(rows, landed_b_ref.shape[0] - rows), :].astype(jnp.float32)
+        sums = [lines[k + 2 : k + 3] + lines[k + 1 : k + 2] + lines[k : k + 1] for k in (0, 3)]
+        gain_out_ref[...] = part_ref[...] + jnp.concatenate(sums, axis=1)
 
     step = 16
 
@@ -586,17 +688,19 @@
         block = pl.ds(pl.multiple_of(i * count + j * step, step), step)
         x = x_ref[block, :].astype(jnp.float32)
         inverse = lax.rsqrt(jnp.mean(x * x, axis=-1, keepdims=True) + epsilon)
-        scaled = (
-            here_ref[block, :].astype(jnp.float32) + landed_ref[block, :].astype(jnp.float32)
-        ) * gain_ref[...]
+        summed = [
+            here[block, :].astype(jnp.float32) + landed[block, :].astype(jnp.float32)
+            for here, landed in ((here_a_ref, landed_a_ref), (here_b_ref, landed_b_ref))
+        ]
+        scaled = jnp.concatenate(summed, axis=1) * gain_ref[...]
         pull = jnp.mean(scaled * x, axis=-1, keepdims=True) * (inverse * inverse)
         out_ref[ds(j, step), :] = (inverse * (scaled - x * pull)).astype(jnp.bfloat16)
         return 0
 
-    lax.fori_loop(0, count // step, some, 0, unroll=2)
-
-
-def pair_body(
+    lax.fori_loop(0, count // step, some, 0, unroll=True)
+
+
+def pair_parts(
     n_rep,
     tokens,
     norm_gain,
@@ -615,52 +719,61 @@
     total = qw + 2 * kw
     frag_rows = local_fragment.shape[1]
     piece_rows = 16
-    piece_cols = width * frag_rows // piece_rows // n_rep
-    chunks = 6
+    n_lanes = n_rep // 2
+    piece_cols = width * frag_rows // piece_rows // n_lanes
+    chunks = 12
     tile = 512
     pad = 8
+    first = width // 2
     bf16, f32 = jnp.bfloat16, jnp.float32
     cosine, sine = host_tables(sequence, HEAD_SIZE)
     vmem = pl.BlockSpec(memory_space=pltpu.VMEM)
     hbm = pl.BlockSpec(memory_space=pltpu.HBM)
-    x, normed, d, here, far, gain_partial, mean_local = pl.pallas_call(
+    x, normed, d, here_a, far_a, gain_a, mean_local, weights = pl.pallas_call(
         functools.partial(front_kernel, n_rep, chunks, tile),
         out_shape=(
             pltpu.VMEM((rows, width), bf16),
             pltpu.VMEM((sequence, width), bf16),
             pltpu.VMEM((sequence, total), bf16),
-            pltpu.VMEM((rows, width), bf16),
-            pltpu.VMEM((rows + pad, width), bf16),
-            pltpu.VMEM((1, width), f32),
+            pltpu.VMEM((rows, first), bf16),
+            pltpu.VMEM((rows, first), bf16),
+            pltpu.VMEM((1, first), f32),
             pltpu.VMEM((frag_rows, width), bf16),
+            pltpu.VMEM((width, total), bf16),
         ),
         in_specs=[hbm] * 9,
-        out_specs=(vmem,) * 7,
+        out_specs=(vmem,) * 8,
         scratch_shapes=[
             pltpu.VMEM((1, width), f32),
             pltpu.VMEM((sequence, qw), bf16),
             pltpu.VMEM((sequence, HEAD_SIZE), f32),
             pltpu.VMEM((sequence, HEAD_SIZE), f32),
-            pltpu.VMEM((width, total), bf16),
             pltpu.VMEM((sequence, total), f32),
             pltpu.VMEM((sequence, qw), bf16),
             pltpu.VMEM((sequence, kw), bf16),
             pltpu.VMEM((sequence, kw), bf16),
-            pltpu.VMEM((n_rep, piece_rows, piece_cols), bf16),
+            pltpu.VMEM((rows, width), bf16),
+            pltpu.VMEM((rows, LANES), f32),
+            pltpu.VMEM((2, SUBLANES, rows), f32),
+            pltpu.VMEM((frag_rows, width), bf16),
+            pltpu.VMEM((frag_rows, width), bf16),
+            pltpu.VMEM((frag_rows, width), bf16),
+            pltpu.VMEM((n_lanes, piece_rows, piece_cols), bf16),
             pltpu.VMEM((piece_rows, piece_cols), bf16),
             pltpu.SemaphoreType.DMA((5,)),
             pltpu.SemaphoreType.DMA((total // tile,)),
             pltpu.SemaphoreType.DMA((chunks,)),
             pltpu.SemaphoreType.DMA((chunks,)),
-            pltpu.SemaphoreType.DMA((n_rep,)),
-            pltpu.SemaphoreType.DMA((n_rep,)),
-            pltpu.SemaphoreType.DMA((n_rep,)),
-            pltpu.SemaphoreType.DMA((n_rep,)),
+            pltpu.SemaphoreType.DMA((n_lanes,)),
+            pltpu.SemaphoreType.DMA((n_lanes,)),
+            pltpu.SemaphoreType.DMA((n_lanes,)),
+            pltpu.SemaphoreType.DMA((n_lanes,)),
+            pltpu.SemaphoreType.DMA((6,)),
             pltpu.SemaphoreType.DMA,
             pltpu.SemaphoreType.REGULAR,
         ],
         compiler_params=pltpu.CompilerParams(
-            collective_id=0, has_side_effects=True, vmem_limit_bytes=48 * 1024 * 1024
+            collective_id=0, has_side_effects=True, vmem_limit_bytes=20 * 1024 * 1024
         ),
     )(
         *[
@@ -679,8 +792,23 @@
         ]
     )
     swap = [(0, 1), (1, 0)]
-    landed = lax.ppermute(far, "tp", swap)
-    wide = 256
+    landed_a = lax.ppermute(far_a, "tp", swap)
+    far_b, here_b, gain_partial = pl.pallas_call(
+        functools.partial(second_kernel, tile),
+        out_shape=(
+            pltpu.VMEM((rows + pad, width - first), bf16),
+            pltpu.VMEM((rows, width - first), bf16),
+            pltpu.VMEM((1, width), f32),
+        ),
+        in_specs=[vmem] * 5,
+        out_specs=(vmem,) * 3,
+        compiler_params=pltpu.CompilerParams(vmem_limit_bytes=8 * 1024 * 1024),
+        cost_estimate=pl.CostEstimate(
+            flops=sequence * width * total, bytes_accessed=width * total, transcendentals=0
+        ),
+    )(d, normed, weights, norm_gain, gain_a)
+    landed_b = lax.ppermute(far_b, "tp", swap)
+    wide = 768
     columns = lambda size: pl.BlockSpec((size, wide), lambda i: (0, i))
     grad_wq, grad_wk, grad_wv, new_global, new_momentum = pl.pallas_call(
         weights_kernel,
@@ -700,12 +828,12 @@
             columns(frag_rows),
             columns(frag_rows),
         ),
-        compiler_params=pltpu.CompilerParams(vmem_limit_bytes=16 * 1024 * 1024),
+        compiler_params=pltpu.CompilerParams(vmem_limit_bytes=28 * 1024 * 1024),
         cost_estimate=pl.CostEstimate(
             flops=2 * sequence * width * total, bytes_accessed=3 * width * total, transcendentals=0
         ),
     )(normed, d, mean_local, global_fragment, momentum)
-    count = 32
+    count = 64
     block = pl.BlockSpec((count, width), lambda i: (i, 0))
     gradient_rows, gains_gradient = pl.pallas_call(
         rows_kernel,
@@ -714,13 +842,13 @@
             jax.ShapeDtypeStruct((rows, width), bf16),
             jax.ShapeDtypeStruct((1, width), f32),
         ),
-        in_specs=[vmem] * 5,
+        in_specs=[vmem] * 7,
         out_specs=(block, pl.BlockSpec((1, width), lambda i: (0, 0))),
         compiler_params=pltpu.CompilerParams(vmem_limit_bytes=8 * 1024 * 1024),
         cost_estimate=pl.CostEstimate(
             flops=12 * rows * width, bytes_accessed=4 * rows * width, transcendentals=0
         ),
-    )(x, here, norm_gain, landed, gain_partial)
+    )(x, here_a, here_b, norm_gain, landed_a, landed_b, gain_partial)
     return (
         grad_wq[None],
         grad_wk[None],
@@ -745,7 +873,7 @@
         P("rep", "tp", None),
     )
     paired = mesh.shape["tp"] == 2 and mesh.shape["rep"] % 2 == 0
-    chosen = functools.partial(pair_body, mesh.shape["rep"]) if paired else body
+    chosen = functools.partial(pair_parts, mesh.shape["rep"]) if paired else body
     return jax.shard_map(
         chosen,
         mesh=mesh,

time: 52.6 us -> 47.2 us (0.90)
  Pallas kernels: 47.8 us -> 39.6 us
  waiting for transfers between devices: 2.71 us -> 5.18 us
    pallas_call x3 -> x4, Pallas kernels: 47.8 us -> 39.6 us  [the longest x1 29.4 us: pair_parts(): pl.pallas_call(functools.partial(front_kernel, n_rep, chunks, tile), out_...]
    ppermute x1 -> x2, waiting for transfers between devices: 2.71 us -> 5.18 us  [the longest x1 5.18 us: pair_parts(): landed_a = lax.ppermute(far_a, 'tp', swap)]
    ppermute x1 -> x2, starting transfers between devices: 1.31 us -> 1.53 us  [the longest x1 1.19 us: pair_parts(): landed_a = lax.ppermute(far_a, 'tp', swap)]
  transfers between devices with their start and end apart: 1 -> 2, of which waited for: 1 -> 1; matrix products, arithmetic and copies ran while one was open for 0% -> 0% of each run, Pallas kernels for 17% -> 14%
where the time goes in v3:
time: 47.2 us; the launch traced here: 47.1 us
  Pallas kernels  39.6 us (84%)
  waiting for transfers between devices  5.18 us (11%)
  starting transfers between devices  1.53 us (3%)
  between operations  0.68 us (1%)
    pallas_call x1, Pallas kernels, pair_parts(): pl.pallas_call(functools.partial(front_kernel, n_rep, chunks, tile), out_...  29.4 us
    pallas_call x1, Pallas kernels, pair_parts(): pl.pallas_call(weights_kernel, grid=(width // wide,), out_shape=(jax.Shap...  6.36 us
    ppermute x1, waiting for transfers between devices, pair_parts(): landed_a = lax.ppermute(far_a, 'tp', swap)  5.18 us
    pallas_call x1, Pallas kernels, pair_parts(): pl.pallas_call(functools.partial(second_kernel, tile), out_shape=(pltpu.V...  2.41 us
    pallas_call x1, Pallas kernels, pair_parts(): pl.pallas_call(rows_kernel, grid=(rows // count,), out_shape=(jax.ShapeDt...  1.52 us
    ppermute x1, starting transfers between devices, pair_parts(): landed_a = lax.ppermute(far_a, 'tp', swap)  1.19 us
  transfers between devices with their start and end apart: 2, of which 1 were waited for; matrix products, arithmetic and copies ran while one was open for 0% of the time, Pallas kernels for 14%

profile of v3, /device:TPU:1, one launch (start us, length us, event | category | flops | bytes accessed | tf_op | source)
XLA Modules:
  0.0 47.1 jit_solution(15507019203881791251)
XLA Ops:
  0.6 0.0 copy-start
  0.6 29.4 %shard_map.162 = (bf16[128,3072]{1,0:T(8,128)(2,1)S(1)}, bf16[256,3072]{1,0:T(8,128)(2,1)S(1)}, bf16[256,2048]{1,0:T(8,128)(2,1)S(1)}, bf16[128,1536]{1,0:T(8,12...) custom-call(bf16[128,3072]{1,0:T(8,128)(2,1)} %bitcast.13, ...), custom_call_target="tpu_custom_call" | custom-call | tf_op jit(solution)/shard_map/pallas_call | solution.py:732
  30.0 0.0 copy-done
  30.0 0.0 copy-start.1
  30.0 0.0 copy-start.2
  30.0 2.4 %shard_map.164 = (bf16[136,1536]{1,0:T(8,128)(2,1)S(1)}, bf16[128,1536]{1,0:T(8,128)(2,1)S(1)}, f32[1,3072]{1,0:T(1,128)S(1)}) custom-call(bf16[256,2048]{1,0:T(8,128)(2,1)S(1)} %get-tuple-element.26.d_ref, bf16[256,3072]{1,0:T(8,128)(2,1)S(1)} %get-tuple-element.25.nm_ref, bf16[3072,2048]{1,0:T(8,128)(2,1)S(1)} %get-tuple-element.33.w_ref, ...), custom_call_target="tpu_custom_call" | custom-call | flops 1610612736 | bytes 6291456 | tf_op jit(solution)/shard_map/pallas_call | solution.py:796
  32.5 0.3 collective-permute-start.1
  32.8 1.2 %collective-permute-start = (bf16[128,1536]{1,0:T(8,128)(2,1)S(1)}, bf16[128,1536]{1,0:T(8,128)(2,1)S(1)}, u32[]{:S(2)}, u32[]{:S(2)}) collective-permute-start(bf16[128,1536]{1,0:T(8,128)(2,1)S(1)} %get-tuple-element.36), channel_id=1, source_target_pairs={{0,1},{1,0},{2,3},{3,2},{4,5},{5,4},{6,7},{7,6},{8,9},{9,8},{10,11... | collective-permute-start | bytes 1179656 | tf_op jit(solution)/shard_map/ppermute | solution.py:795
  34.0 0.0 copy-done.1
  34.0 0.0 copy-done.2
  34.0 6.4 %shard_map.163 = (bf16[3072,1024]{1,0:T(8,128)(2,1)}, bf16[3072,512]{1,0:T(8,128)(2,1)}, bf16[3072,512]{1,0:T(8,128)(2,1)}, f32[64,3072]{1,0:T(8,128)}, f32[64,3072]{1,0:T(8,128)}) custom-call(bf16[256,3072]{1,0:T(8,128)(2,1)S(1)} %get-tuple-element.25.nm_ref, bf16[256,2048]{1,0:T(8,128)(2,1)S(1)} %get-tuple-element.26.d_ref, ...), custom_call_target="tpu_custom_call" | custom-call | flops 3221225472 | bytes 18874368 | tf_op jit(solution)/shard_map/pallas_call | solution.py:813
  40.4 5.2 %collective-permute-done.landed_a_ref = bf16[128,1536]{1,0:T(8,128)(2,1)S(1)} collective-permute-done((bf16[128,1536]{1,0:T(8,128)(2,1)S(1)}, bf16[128,1536]{1,0:T(8,128)(2,1)S(1)}, u32[]{:S(2)}, u32[]{:S(2)}) %collective-permute-start) | collective-permute-done | bytes 393248 | tf_op jit(solution)/shard_map/ppermute | solution.py:795
  45.5 0.0 collective-permute-done.1.landed_b_ref
  45.5 1.5 %shard_map.165 = (bf16[128,3072]{1,0:T(8,128)(2,1)}, f32[1,3072]{1,0:T(1,128)}) custom-call(bf16[128,3072]{1,0:T(8,128)(2,1)S(1)} %get-tuple-element.31.x_ref, bf16[128,1536]{1,0:T(8,128)(2,1)S(1)} %get-tuple-element.32.here_a_ref, bf16[128,1536]{1,0:T(8,128)(2,1)S(1)} %get-tuple-element.35.here_b_ref, f32[1,3072]{1,0:T(1,128)S(1)} %copy-done, ...), custom_call_target="tpu_custom_call" | custom-call | flops 4718592 | bytes 1572864 | tf_op jit(solution)/shard_map/pallas_call | solution.py:838
Async XLA Ops:
  0.6 29.4 %copy-start = (f32[1,3072]{1,0:T(1,128)S(1)}, f32[1,3072]{1,0:T(1,128)}, u32[]{:S(2)}) copy-start(f32[1,3072]{1,0:T(1,128)} %gain_ref.3) | copy-start | bytes 36868
  30.0 4.0 %copy-start.1 = (f32[64,3072]{1,0:T(8,128)S(1)}, f32[64,3072]{1,0:T(8,128)}, u32[]{:S(2)}) copy-start(f32[64,3072]{1,0:T(8,128)} %global_ref.1) | copy-start | bytes 2359300
  30.0 4.0 %copy-start.2 = (f32[64,3072]{1,0:T(8,128)S(1)}, f32[64,3072]{1,0:T(8,128)}, u32[]{:S(2)}) copy-start(f32[64,3072]{1,0:T(8,128)} %momentum_ref.1) | copy-start | bytes 2359300
  32.5 13.1 %collective-permute-start.1 = (bf16[136,1536]{1,0:T(8,128)(2,1)S(1)}, bf16[136,1536]{1,0:T(8,128)(2,1)S(1)}, u32[]{:S(2)}, u32[]{:S(2)}) collective-permute-start(bf16[136,1536]{1,0:T(8,128)(2,1)S(1)} %get-tuple-element.37), channel_id=1, source_target_pairs={{0,1},{1,0},{2,3},{3,2},{4,5},{5,4},{6,7},{7,6},{8,9},{9,8},{10,11... | collective-permute-start | bytes 1253384 | tf_op jit(solution)/shard_map/ppermute | solution.py:810
  32.8 12.7 %collective-permute-start = (bf16[128,1536]{1,0:T(8,128)(2,1)S(1)}, bf16[128,1536]{1,0:T(8,128)(2,1)S(1)}, u32[]{:S(2)}, u32[]{:S(2)}) collective-permute-start(bf16[128,1536]{1,0:T(8,128)(2,1)S(1)} %get-tuple-element.36), channel_id=1, source_target_pairs={{0,1},{1,0},{2,3},{3,2},{4,5},{5,4},{6,7},{7,6},{8,9},{9,8},{10,11... | collective-permute-start | bytes 1179656 | tf_op jit(solution)/shard_map/ppermute | solution.py:795

commit v4 on v3

--- a/solution.py
+++ b/solution.py
@@ -252,7 +252,7 @@
         gain_part_ref[:, pl.ds(pl.multiple_of(offset + t * tile, tile), tile)] = gain_part
         return 0
 
-    lax.fori_loop(0, here_ref.shape[1] // tile, back, 0)
+    lax.fori_loop(0, here_ref.shape[1] // tile, back, 0, unroll=True)
 
 
 def front_kernel(
@@ -361,9 +361,9 @@
         half_copy.start()
 
 
-    def gather_copy(c):
+    def gather_copy(c, source=x_ref):
         return pltpu.make_async_remote_copy(
-            src_ref=tokens_hbm.at[:, ds(c, cw)],
+            src_ref=source.at[:, ds(c, cw)],
             dst_ref=raw_ref.at[:, ds(c, cw)],
             send_sem=ag_send.at[c],
             recv_sem=ag_recv.at[c],
@@ -445,15 +445,16 @@
         lax.fori_loop(low, high, one, 0)
 
     early = chunks // 3
-    pl.semaphore_wait(barrier, 2 + side * (n_lanes - 1))
 
     @pl.when(side == 0)
     def _():
-        start_all(gather_copy, 0, early)
+        pl.semaphore_wait(barrier, 2)
+        start_all(lambda c: gather_copy(c, tokens_hbm), 0, early)
         pair_copy.start()
 
     for copy in first_copies:
         copy.wait()
+
     for copy in weight_copies + late_copies:
         copy.start()
 
@@ -468,8 +469,13 @@
         ).astype(jnp.bfloat16)
         return 0
 
-    lax.fori_loop(0, rows // step, norm_rows, 0)
+    lax.fori_loop(0, rows // step, norm_rows, 0, unroll=2)
     inv_ref[0] = wide_ref[...].T[:SUBLANES]
+
+    @pl.when(side == 1)
+    def _():
+        pl.semaphore_wait(barrier, n_lanes + 1)
+
     norm_copy.start()
 
     @pl.when(side == 0)
@@ -541,11 +547,11 @@
     def arrived(c, _):
         gather_copy(c).wait_recv()
 
-        @pl.when((side == 0) & (c == chunks - 4))
+        @pl.when((side == 0) & (c == chunks - 5))
         def _():
             pl.semaphore_signal(go_sem, inc=1, device_id={"rep": partner}, device_id_type=MESH)
 
-        @pl.when((side == 1) & (c == chunks - 5))
+        @pl.when((side == 1) & (c == chunks - 8))
         def _():
             pass_mean()
 
@@ -578,46 +584,58 @@
         s = sin_ref[block * rows : (block + 1) * rows]
         return (gradient * c - pltpu.roll(gradient, HEAD_SIZE // 2, 1) * s).astype(jnp.bfloat16)
 
-    def kv_head(g, _):
-        grad_k = [None, None]
-        grad_v = [None, None]
-        kv = ds(g, HEAD_SIZE)
+    def kv_heads(low):
+        members = range(low, low + 4)
+        grads = {}
         for b in range(2):
             keys = (b + 1) * rows
             block = pl.ds(b * rows, rows)
-            heads = [ds(g * group + r, HEAD_SIZE) for r in range(group)]
-            query = jnp.concatenate([q_ref[block, head] for head in heads], axis=0)
-            out_grad = jnp.concatenate([go_ref[block, head] for head in heads], axis=0)
-            key = k_ref[pl.ds(0, keys), kv]
-            value = v_ref[pl.ds(0, keys), kv]
-            scores = dot(key, query, NT)
-            grad_prob = dot(value, out_grad, NT)
-            if b == 0:
-                scores = scores + bias
-            else:
-                scores = jnp.concatenate([scores[:rows], scores[rows:] + bias], axis=0)
-            highest = jnp.max(scores, axis=0, keepdims=True)
-            powers = jnp.exp2((scores - highest) * (scale * LOG2_E))
-            prob = powers * (1.0 / jnp.sum(powers, axis=0, keepdims=True))
-            inner = jnp.sum(grad_prob * prob, axis=0, keepdims=True)
-            score_low = (prob * (grad_prob - inner) * scale).astype(jnp.bfloat16)
-            grad_q = dot(score_low, key, TN)
-            for r, head in enumerate(heads):
-                d_ref[block, head] = reverse(grad_q[r * rows : (r + 1) * rows], b)
-            part_v = dot(prob.astype(jnp.bfloat16), out_grad)
-            part_k = dot(score_low, query)
-            for j in range(b + 1):
-                pv = part_v[j * rows : (j + 1) * rows]
-                pk = part_k[j * rows : (j + 1) * rows]
-                grad_v[j] = pv if grad_v[j] is None else grad_v[j] + pv
-                grad_k[j] = pk if grad_k[j] is None else grad_k[j] + pk
-        for j in range(2):
-            block = pl.ds(j * rows, rows)
-            d_ref[block, ds(heads_q + g, HEAD_SIZE)] = reverse(grad_k[j], j)
-            d_ref[block, ds(heads_q + heads_kv + g, HEAD_SIZE)] = grad_v[j].astype(jnp.bfloat16)
-        return 0
-
-    lax.fori_loop(0, heads_kv, kv_head, 0, unroll=True)
+            loaded, dots, soft = {}, {}, {}
+            for g in members:
+                heads = [pl.ds((g * group + r) * HEAD_SIZE, HEAD_SIZE) for r in range(group)]
+                kv = pl.ds(g * HEAD_SIZE, HEAD_SIZE)
+                query = jnp.concatenate([q_ref[block, head] for head in heads], axis=0)
+                out_grad = jnp.concatenate([go_ref[block, head] for head in heads], axis=0)
+                key = k_ref[pl.ds(0, keys), kv]
+                value = v_ref[pl.ds(0, keys), kv]
+                loaded[g] = heads, query, out_grad, key
+                dots[g] = dot(key, query, NT), dot(value, out_grad, NT)
+            for g in members:
+                scores, grad_prob = dots[g]
+                if b == 0:
+                    scores = scores + bias
+                else:
+                    scores = jnp.concatenate([scores[:rows], scores[rows:] + bias], axis=0)
+                highest = jnp.max(scores, axis=0, keepdims=True)
+                powers = jnp.exp2((scores - highest) * (scale * LOG2_E))
+                prob = powers * (1.0 / jnp.sum(powers, axis=0, keepdims=True))
+                inner = jnp.sum(grad_prob * prob, axis=0, keepdims=True)
+                score_low = (prob * (grad_prob - inner) * scale).astype(jnp.bfloat16)
+                soft[g] = prob.astype(jnp.bfloat16), score_low
+            for g in members:
+                heads, query, out_grad, key = loaded[g]
+                prob_low, score_low = soft[g]
+                part_v = dot(prob_low, out_grad)
+                part_k = dot(score_low, query)
+                grad_q = dot(score_low, key, TN)
+                for r, head in enumerate(heads):
+                    d_ref[block, head] = reverse(grad_q[r * rows : (r + 1) * rows], b)
+                for j in range(b + 1):
+                    pv = part_v[j * rows : (j + 1) * rows]
+                    pk = part_k[j * rows : (j + 1) * rows]
+                    if (g, j) in grads:
+                        pv, pk = pv + grads[g, j][0], pk + grads[g, j][1]
+                    grads[g, j] = pv, pk
+        for g in members:
+            for j in range(2):
+                block = pl.ds(j * rows, rows)
+                low_k = (heads_q + g) * HEAD_SIZE
+                d_ref[block, pl.ds(low_k, HEAD_SIZE)] = reverse(grads[g, j][1], j)
+                low_v = (heads_q + heads_kv + g) * HEAD_SIZE
+                d_ref[block, pl.ds(low_v, HEAD_SIZE)] = grads[g, j][0].astype(jnp.bfloat16)
+
+    for low in range(0, heads_kv, 4):
+        kv_heads(low)
 
     shares(d_ref, nm_ref, w_ref, gain_ref, far_ref, here_ref, gain_part_ref, 0, tile)
 
@@ -833,7 +851,7 @@
             flops=2 * sequence * width * total, bytes_accessed=3 * width * total, transcendentals=0
         ),
     )(normed, d, mean_local, global_fragment, momentum)
-    count = 64
+    count = rows // 2
     block = pl.BlockSpec((count, width), lambda i: (i, 0))
     gradient_rows, gains_gradient = pl.pallas_call(
         rows_kernel,

time: 47.2 us -> 44 us (0.932)
  Pallas kernels: 39.6 us -> 36.7 us
    pallas_call x1, Pallas kernels: 29.4 us -> 26.8 us  [pair_parts(): pl.pallas_call(functools.partial(front_kernel, n_rep, chunks, tile), out_...]
    ppermute x1, starting transfers between devices: 1.19 us -> 0.29 us  [pair_parts(): landed_a = lax.ppermute(far_a, 'tp', swap)]
    ppermute x1, starting transfers between devices: 0.34 us -> 1.24 us  [pair_parts(): landed_b = lax.ppermute(far_b, 'tp', swap)]
  transfers between devices with their start and end apart: 2 -> 2, of which waited for: 1 -> 1; matrix products, arithmetic and copies ran while one was open for 0% -> 0% of each run, Pallas kernels for 14% -> 15%
where the time goes in v4:
time: 44 us; the launch traced here: 43.8 us
  Pallas kernels  36.7 us (83%)
  waiting for transfers between devices  4.92 us (11%)
  starting transfers between devices  1.53 us (3%)
  between operations  0.68 us (2%)
    pallas_call x1, Pallas kernels, pair_parts(): pl.pallas_call(functools.partial(front_kernel, n_rep, chunks, tile), out_...  26.8 us
    pallas_call x1, Pallas kernels, pair_parts(): pl.pallas_call(weights_kernel, grid=(width // wide,), out_shape=(jax.Shap...  6.35 us
    ppermute x1, waiting for transfers between devices, pair_parts(): landed_a = lax.ppermute(far_a, 'tp', swap)  4.92 us
    pallas_call x1, Pallas kernels, pair_parts(): pl.pallas_call(functools.partial(second_kernel, tile), out_shape=(pltpu.V...  2 us
    pallas_call x1, Pallas kernels, pair_parts(): pl.pallas_call(rows_kernel, grid=(rows // count,), out_shape=(jax.ShapeDt...  1.52 us
    ppermute x1, starting transfers between devices, pair_parts(): landed_b = lax.ppermute(far_b, 'tp', swap)  1.24 us
  transfers between devices with their start and end apart: 2, of which 1 were waited for; matrix products, arithmetic and copies ran while one was open for 0% of the time, Pallas kernels for 15%

profile of v4, /device:TPU:1, one launch (start us, length us, event | category | flops | bytes accessed | tf_op | source)
XLA Modules:
  0.0 43.8 jit_solution(15377168067836992748)
XLA Ops:
  0.6 0.0 copy-start
  0.6 26.8 %shard_map.162 = (bf16[128,3072]{1,0:T(8,128)(2,1)S(1)}, bf16[256,3072]{1,0:T(8,128)(2,1)S(1)}, bf16[256,2048]{1,0:T(8,128)(2,1)S(1)}, bf16[128,1536]{1,0:T(8,12...) custom-call(bf16[128,3072]{1,0:T(8,128)(2,1)} %bitcast.13, ...), custom_call_target="tpu_custom_call" | custom-call | tf_op jit(solution)/shard_map/pallas_call | solution.py:750
  27.5 0.0 copy-done
  27.5 0.0 copy-start.1
  27.5 0.0 copy-start.2
  27.5 2.0 %shard_map.164 = (bf16[136,1536]{1,0:T(8,128)(2,1)S(1)}, bf16[128,1536]{1,0:T(8,128)(2,1)S(1)}, f32[1,3072]{1,0:T(1,128)S(1)}) custom-call(bf16[256,2048]{1,0:T(8,128)(2,1)S(1)} %get-tuple-element.26.d_ref, bf16[256,3072]{1,0:T(8,128)(2,1)S(1)} %get-tuple-element.25.nm_ref, bf16[3072,2048]{1,0:T(8,128)(2,1)S(1)} %get-tuple-element.33.w_ref, ...), custom_call_target="tpu_custom_call" | custom-call | flops 1610612736 | bytes 6291456 | tf_op jit(solution)/shard_map/pallas_call | solution.py:814
  29.5 1.2 %collective-permute-start.1 = (bf16[136,1536]{1,0:T(8,128)(2,1)S(1)}, bf16[136,1536]{1,0:T(8,128)(2,1)S(1)}, u32[]{:S(2)}, u32[]{:S(2)}) collective-permute-start(bf16[136,1536]{1,0:T(8,128)(2,1)S(1)} %get-tuple-element.37), channel_id=1, source_target_pairs={{0,1},{1,0},{2,3},{3,2},{4,5},{5,4},{6,7},{7,6},{8,9},{9,8},{10,11... | collective-permute-start | bytes 1253384 | tf_op jit(solution)/shard_map/ppermute | solution.py:828
  30.7 0.3 collective-permute-start
  31.0 0.0 copy-done.1
  31.0 0.0 copy-done.2
  31.0 6.4 %shard_map.163 = (bf16[3072,1024]{1,0:T(8,128)(2,1)}, bf16[3072,512]{1,0:T(8,128)(2,1)}, bf16[3072,512]{1,0:T(8,128)(2,1)}, f32[64,3072]{1,0:T(8,128)}, f32[64,3072]{1,0:T(8,128)}) custom-call(bf16[256,3072]{1,0:T(8,128)(2,1)S(1)} %get-tuple-element.25.nm_ref, bf16[256,2048]{1,0:T(8,128)(2,1)S(1)} %get-tuple-element.26.d_ref, ...), custom_call_target="tpu_custom_call" | custom-call | flops 3221225472 | bytes 18874368 | tf_op jit(solution)/shard_map/pallas_call | solution.py:831
  37.4 4.9 %collective-permute-done.landed_a_ref = bf16[128,1536]{1,0:T(8,128)(2,1)S(1)} collective-permute-done((bf16[128,1536]{1,0:T(8,128)(2,1)S(1)}, bf16[128,1536]{1,0:T(8,128)(2,1)S(1)}, u32[]{:S(2)}, u32[]{:S(2)}) %collective-permute-start) | collective-permute-done | bytes 393248 | tf_op jit(solution)/shard_map/ppermute | solution.py:813
  42.3 0.0 collective-permute-done.1.landed_b_ref
  42.3 1.5 %shard_map.165 = (bf16[128,3072]{1,0:T(8,128)(2,1)}, f32[1,3072]{1,0:T(1,128)}) custom-call(bf16[128,3072]{1,0:T(8,128)(2,1)S(1)} %get-tuple-element.31.x_ref, bf16[128,1536]{1,0:T(8,128)(2,1)S(1)} %get-tuple-element.32.here_a_ref, bf16[128,1536]{1,0:T(8,128)(2,1)S(1)} %get-tuple-element.35.here_b_ref, f32[1,3072]{1,0:T(1,128)S(1)} %copy-done, ...), custom_call_target="tpu_custom_call" | custom-call | flops 4718592 | bytes 1572864 | tf_op jit(solution)/shard_map/pallas_call | solution.py:856
Async XLA Ops:
  0.6 26.8 %copy-start = (f32[1,3072]{1,0:T(1,128)S(1)}, f32[1,3072]{1,0:T(1,128)}, u32[]{:S(2)}) copy-start(f32[1,3072]{1,0:T(1,128)} %gain_ref.3) | copy-start | bytes 36868
  27.5 3.6 %copy-start.1 = (f32[64,3072]{1,0:T(8,128)S(1)}, f32[64,3072]{1,0:T(8,128)}, u32[]{:S(2)}) copy-start(f32[64,3072]{1,0:T(8,128)} %global_ref.1) | copy-start | bytes 2359300
  27.5 3.6 %copy-start.2 = (f32[64,3072]{1,0:T(8,128)S(1)}, f32[64,3072]{1,0:T(8,128)}, u32[]{:S(2)}) copy-start(f32[64,3072]{1,0:T(8,128)} %momentum_ref.1) | copy-start | bytes 2359300
  29.5 12.8 %collective-permute-start.1 = (bf16[136,1536]{1,0:T(8,128)(2,1)S(1)}, bf16[136,1536]{1,0:T(8,128)(2,1)S(1)}, u32[]{:S(2)}, u32[]{:S(2)}) collective-permute-start(bf16[136,1536]{1,0:T(8,128)(2,1)S(1)} %get-tuple-element.37), channel_id=1, source_target_pairs={{0,1},{1,0},{2,3},{3,2},{4,5},{5,4},{6,7},{7,6},{8,9},{9,8},{10,11... | collective-permute-start | bytes 1253384 | tf_op jit(solution)/shard_map/ppermute | solution.py:828
  30.7 11.6 %collective-permute-start = (bf16[128,1536]{1,0:T(8,128)(2,1)S(1)}, bf16[128,1536]{1,0:T(8,128)(2,1)S(1)}, u32[]{:S(2)}, u32[]{:S(2)}) collective-permute-start(bf16[128,1536]{1,0:T(8,128)(2,1)S(1)} %get-tuple-element.36), channel_id=1, source_target_pairs={{0,1},{1,0},{2,3},{3,2},{4,5},{5,4},{6,7},{7,6},{8,9},{9,8},{10,11... | collective-permute-start | bytes 1179656 | tf_op jit(solution)/shard_map/ppermute | solution.py:813

commit v5 on v4

--- a/solution.py
+++ b/solution.py
@@ -365,7 +365,7 @@
         return pltpu.make_async_remote_copy(
             src_ref=source.at[:, ds(c, cw)],
             dst_ref=raw_ref.at[:, ds(c, cw)],
-            send_sem=ag_send.at[c],
+            send_sem=ag_send,
             recv_sem=ag_recv.at[c],
             device_id={"tp": peer},
             device_id_type=MESH,
@@ -407,8 +407,8 @@
         return pltpu.make_async_remote_copy(
             src_ref=pair_ref.at[piece(lax.rem(lane + j, n_lanes))],
             dst_ref=pieces_ref.at[j],
-            send_sem=fr_send.at[j],
-            recv_sem=fr_recv.at[j],
+            send_sem=fr_send,
+            recv_sem=fr_recv,
             device_id={"rep": along(j)},
             device_id_type=MESH,
         )
@@ -417,29 +417,30 @@
         return pltpu.make_async_remote_copy(
             src_ref=own_mean_ref,
             dst_ref=mean_ref.at[piece(owner)],
-            send_sem=fg_send.at[j],
-            recv_sem=fg_recv.at[j],
+            send_sem=fg_send,
+            recv_sem=fg_recv,
             device_id={"rep": along(j)},
             device_id_type=MESH,
         )
+
+    def all_of(part, send_sem, recv_sem):
+        return pltpu.make_async_remote_copy(
+            src_ref=part,
+            dst_ref=part,
+            send_sem=send_sem,
+            recv_sem=recv_sem,
+            device_id={"rep": partner},
+            device_id_type=MESH,
+        )
+
+    others = pieces_ref.at[pl.ds(1, n_lanes - 1)]
+    all_scattered = all_of(others, fr_send, fr_recv)
+    all_spread = all_of(others, fg_send, fg_recv)
+    all_gathered = all_of(x_ref, ag_send, own_sem)
 
     def start_all(make, low, high):
         def one(j, _):
             make(j).start()
-            return 0
-
-        lax.fori_loop(low, high, one, 0)
-
-    def wait_recv_all(make, low, high):
-        def one(j, _):
-            make(j).wait_recv()
-            return 0
-
-        lax.fori_loop(low, high, one, 0)
-
-    def wait_send_all(make, low, high):
-        def one(j, _):
-            make(j).wait_send()
             return 0
 
         lax.fori_loop(low, high, one, 0)
@@ -520,7 +521,7 @@
     rope_rows(me)
 
     def average_pieces():
-        wait_recv_all(scatter_copy, 1, n_lanes)
+        all_scattered.wait_recv()
         summed = pair_ref[piece(lane)].astype(jnp.float32)
         for j in range(1, n_lanes):
             summed = summed + pieces_ref[j].astype(jnp.float32)
@@ -530,9 +531,7 @@
         start_all(lambda j: spread_copy(j, lane), 1, n_lanes)
 
     def pass_mean():
-        wait_recv_all(
-            lambda j: spread_copy(j, lax.rem(lane + n_lanes - j, n_lanes)), 1, n_lanes
-        )
+        all_spread.wait_recv()
         mean_copy.start()
 
     @pl.when(side == 1)
@@ -640,7 +639,7 @@
     shares(d_ref, nm_ref, w_ref, gain_ref, far_ref, here_ref, gain_part_ref, 0, tile)
 
     norm_copy.wait_send()
-    wait_send_all(gather_copy, 0, chunks)
+    all_gathered.wait_send()
 
     @pl.when(side == 0)
     def _():
@@ -649,8 +648,8 @@
 
     @pl.when(side == 1)
     def _():
-        wait_send_all(scatter_copy, 1, n_lanes)
-        wait_send_all(lambda j: spread_copy(j, lane), 1, n_lanes)
+        all_scattered.wait_send()
+        all_spread.wait_send()
         mean_copy.wait_send()
 
 
@@ -780,12 +779,12 @@
             pltpu.VMEM((piece_rows, piece_cols), bf16),
             pltpu.SemaphoreType.DMA((5,)),
             pltpu.SemaphoreType.DMA((total // tile,)),
+            pltpu.SemaphoreType.DMA,
             pltpu.SemaphoreType.DMA((chunks,)),
-            pltpu.SemaphoreType.DMA((chunks,)),
-            pltpu.SemaphoreType.DMA((n_lanes,)),
-            pltpu.SemaphoreType.DMA((n_lanes,)),
-            pltpu.SemaphoreType.DMA((n_lanes,)),
-            pltpu.SemaphoreType.DMA((n_lanes,)),
+            pltpu.SemaphoreType.DMA,
+            pltpu.SemaphoreType.DMA,
+            pltpu.SemaphoreType.DMA,
+            pltpu.SemaphoreType.DMA,
             pltpu.SemaphoreType.DMA((6,)),
             pltpu.SemaphoreType.DMA,
             pltpu.SemaphoreType.REGULAR,

time: 44 us -> 43.5 us (0.989)
  Pallas kernels: 36.7 us -> 36.2 us
    pallas_call x1, Pallas kernels: 26.8 us -> 26.3 us  [pair_parts(): pl.pallas_call(functools.partial(front_kernel, n_rep, chunks, tile), out_...]
where the time goes in v5:
time: 43.5 us; the launch traced here: 43.4 us
  Pallas kernels  36.2 us (83%)
  waiting for transfers between devices  4.98 us (11%)
  starting transfers between devices  1.53 us (4%)
  between operations  0.68 us (2%)
    pallas_call x1, Pallas kernels, pair_parts(): pl.pallas_call(functools.partial(front_kernel, n_rep, chunks, tile), out_...  26.3 us
    pallas_call x1, Pallas kernels, pair_parts(): pl.pallas_call(weights_kernel, grid=(width // wide,), out_shape=(jax.Shap...  6.36 us
    ppermute x1, waiting for transfers between devices, pair_parts(): landed_a = lax.ppermute(far_a, 'tp', swap)  4.98 us
    pallas_call x1, Pallas kernels, pair_parts(): pl.pallas_call(functools.partial(second_kernel, tile), out_shape=(pltpu.V...  1.99 us
    pallas_call x1, Pallas kernels, pair_parts(): pl.pallas_call(rows_kernel, grid=(rows // count,), out_shape=(jax.ShapeDt...  1.52 us
    ppermute x1, starting transfers between devices, pair_parts(): landed_b = lax.ppermute(far_b, 'tp', swap)  1.25 us
  transfers between devices with their start and end apart: 2, of which 1 were waited for; matrix products, arithmetic and copies ran while one was open for 0% of the time, Pallas kernels for 15%

profile of v5, /device:TPU:1, one launch (start us, length us, event | category | flops | bytes accessed | tf_op | source)
XLA Modules:
  0.0 43.4 jit_solution(4529690500522952117)
XLA Ops:
  0.6 0.0 copy-start
  0.6 26.3 %shard_map.162 = (bf16[128,3072]{1,0:T(8,128)(2,1)S(1)}, bf16[256,3072]{1,0:T(8,128)(2,1)S(1)}, bf16[256,2048]{1,0:T(8,128)(2,1)S(1)}, bf16[128,1536]{1,0:T(8,12...) custom-call(bf16[128,3072]{1,0:T(8,128)(2,1)} %bitcast.13, ...), custom_call_target="tpu_custom_call" | custom-call | tf_op jit(solution)/shard_map/pallas_call | solution.py:749
  27.0 0.0 copy-done
  27.0 0.0 copy-start.1
  27.0 0.0 copy-start.2
  27.0 2.0 %shard_map.164 = (bf16[136,1536]{1,0:T(8,128)(2,1)S(1)}, bf16[128,1536]{1,0:T(8,128)(2,1)S(1)}, f32[1,3072]{1,0:T(1,128)S(1)}) custom-call(bf16[256,2048]{1,0:T(8,128)(2,1)S(1)} %get-tuple-element.26.d_ref, bf16[256,3072]{1,0:T(8,128)(2,1)S(1)} %get-tuple-element.25.nm_ref, bf16[3072,2048]{1,0:T(8,128)(2,1)S(1)} %get-tuple-element.33.w_ref, ...), custom_call_target="tpu_custom_call" | custom-call | flops 1610612736 | bytes 6291456 | tf_op jit(solution)/shard_map/pallas_call | solution.py:813
  29.0 1.3 %collective-permute-start.1 = (bf16[136,1536]{1,0:T(8,128)(2,1)S(1)}, bf16[136,1536]{1,0:T(8,128)(2,1)S(1)}, u32[]{:S(2)}, u32[]{:S(2)}) collective-permute-start(bf16[136,1536]{1,0:T(8,128)(2,1)S(1)} %get-tuple-element.37), channel_id=1, source_target_pairs={{0,1},{1,0},{2,3},{3,2},{4,5},{5,4},{6,7},{7,6},{8,9},{9,8},{10,11... | collective-permute-start | bytes 1253384 | tf_op jit(solution)/shard_map/ppermute | solution.py:827
  30.3 0.3 collective-permute-start
  30.5 0.0 copy-done.1
  30.5 0.0 copy-done.2
  30.5 6.4 %shard_map.163 = (bf16[3072,1024]{1,0:T(8,128)(2,1)}, bf16[3072,512]{1,0:T(8,128)(2,1)}, bf16[3072,512]{1,0:T(8,128)(2,1)}, f32[64,3072]{1,0:T(8,128)}, f32[64,3072]{1,0:T(8,128)}) custom-call(bf16[256,3072]{1,0:T(8,128)(2,1)S(1)} %get-tuple-element.25.nm_ref, bf16[256,2048]{1,0:T(8,128)(2,1)S(1)} %get-tuple-element.26.d_ref, ...), custom_call_target="tpu_custom_call" | custom-call | flops 3221225472 | bytes 18874368 | tf_op jit(solution)/shard_map/pallas_call | solution.py:830
  36.9 5.0 %collective-permute-done.landed_a_ref = bf16[128,1536]{1,0:T(8,128)(2,1)S(1)} collective-permute-done((bf16[128,1536]{1,0:T(8,128)(2,1)S(1)}, bf16[128,1536]{1,0:T(8,128)(2,1)S(1)}, u32[]{:S(2)}, u32[]{:S(2)}) %collective-permute-start) | collective-permute-done | bytes 393248 | tf_op jit(solution)/shard_map/ppermute | solution.py:812
  41.9 0.0 collective-permute-done.1.landed_b_ref
  41.9 1.5 %shard_map.165 = (bf16[128,3072]{1,0:T(8,128)(2,1)}, f32[1,3072]{1,0:T(1,128)}) custom-call(bf16[128,3072]{1,0:T(8,128)(2,1)S(1)} %get-tuple-element.31.x_ref, bf16[128,1536]{1,0:T(8,128)(2,1)S(1)} %get-tuple-element.32.here_a_ref, bf16[128,1536]{1,0:T(8,128)(2,1)S(1)} %get-tuple-element.35.here_b_ref, f32[1,3072]{1,0:T(1,128)S(1)} %copy-done, ...), custom_call_target="tpu_custom_call" | custom-call | flops 4718592 | bytes 1572864 | tf_op jit(solution)/shard_map/pallas_call | solution.py:855
Async XLA Ops:
  0.6 26.3 %copy-start = (f32[1,3072]{1,0:T(1,128)S(1)}, f32[1,3072]{1,0:T(1,128)}, u32[]{:S(2)}) copy-start(f32[1,3072]{1,0:T(1,128)} %gain_ref.3) | copy-start | bytes 36868
  27.0 3.6 %copy-start.1 = (f32[64,3072]{1,0:T(8,128)S(1)}, f32[64,3072]{1,0:T(8,128)}, u32[]{:S(2)}) copy-start(f32[64,3072]{1,0:T(8,128)} %global_ref.1) | copy-start | bytes 2359300
  27.0 3.5 %copy-start.2 = (f32[64,3072]{1,0:T(8,128)S(1)}, f32[64,3072]{1,0:T(8,128)}, u32[]{:S(2)}) copy-start(f32[64,3072]{1,0:T(8,128)} %momentum_ref.1) | copy-start | bytes 2359300
  29.0 12.9 %collective-permute-start.1 = (bf16[136,1536]{1,0:T(8,128)(2,1)S(1)}, bf16[136,1536]{1,0:T(8,128)(2,1)S(1)}, u32[]{:S(2)}, u32[]{:S(2)}) collective-permute-start(bf16[136,1536]{1,0:T(8,128)(2,1)S(1)} %get-tuple-element.37), channel_id=1, source_target_pairs={{0,1},{1,0},{2,3},{3,2},{4,5},{5,4},{6,7},{7,6},{8,9},{9,8},{10,11... | collective-permute-start | bytes 1253384 | tf_op jit(solution)/shard_map/ppermute | solution.py:827
  30.3 11.6 %collective-permute-start = (bf16[128,1536]{1,0:T(8,128)(2,1)S(1)}, bf16[128,1536]{1,0:T(8,128)(2,1)S(1)}, u32[]{:S(2)}, u32[]{:S(2)}) collective-permute-start(bf16[128,1536]{1,0:T(8,128)(2,1)S(1)} %get-tuple-element.36), channel_id=1, source_target_pairs={{0,1},{1,0},{2,3},{3,2},{4,5},{5,4},{6,7},{7,6},{8,9},{9,8},{10,11... | collective-permute-start | bytes 1179656 | tf_op jit(solution)/shard_map/ppermute | solution.py:812

commit v6 on v5

--- a/solution.py
+++ b/solution.py
@@ -450,11 +450,20 @@
     @pl.when(side == 0)
     def _():
         pl.semaphore_wait(barrier, 2)
-        start_all(lambda c: gather_copy(c, tokens_hbm), 0, early)
+
+        @pl.when(me == 1)
+        def _():
+            start_all(lambda c: gather_copy(c, tokens_hbm), 0, early)
+
         pair_copy.start()
 
     for copy in first_copies:
         copy.wait()
+
+
+    @pl.when((side == 0) & (me == 0))
+    def _():
+        start_all(gather_copy, 0, early)
 
     for copy in weight_copies + late_copies:
         copy.start()
@@ -699,7 +708,7 @@
         sums = [lines[k + 2 : k + 3] + lines[k + 1 : k + 2] + lines[k : k + 1] for k in (0, 3)]
         gain_out_ref[...] = part_ref[...] + jnp.concatenate(sums, axis=1)
 
-    step = 16
+    step = 8
 
     def some(j, _):
         block = pl.ds(pl.multiple_of(i * count + j * step, step), step)

time: 43.5 us -> 43.4 us (level)
  no operation moved by 1% of the time
where the time goes in v6:
time: 43.4 us; the launch traced here: 43.3 us
  Pallas kernels  36 us (83%)
  waiting for transfers between devices  5.09 us (12%)
  starting transfers between devices  1.53 us (4%)
  between operations  0.68 us (2%)
    pallas_call x1, Pallas kernels, pair_parts(): pl.pallas_call(functools.partial(front_kernel, n_rep, chunks, tile), out_...  26.1 us
    pallas_call x1, Pallas kernels, pair_parts(): pl.pallas_call(weights_kernel, grid=(width // wide,), out_shape=(jax.Shap...  6.36 us
    ppermute x1, waiting for transfers between devices, pair_parts(): landed_a = lax.ppermute(far_a, 'tp', swap)  5.09 us
    pallas_call x1, Pallas kernels, pair_parts(): pl.pallas_call(functools.partial(second_kernel, tile), out_shape=(pltpu.V...  1.99 us
    pallas_call x1, Pallas kernels, pair_parts(): pl.pallas_call(rows_kernel, grid=(rows // count,), out_shape=(jax.ShapeDt...  1.5 us
    ppermute x1, starting transfers between devices, pair_parts(): landed_b = lax.ppermute(far_b, 'tp', swap)  1.25 us
  transfers between devices with their start and end apart: 2, of which 1 were waited for; matrix products, arithmetic and copies ran while one was open for 0% of the time, Pallas kernels for 15%

profile of v6, /device:TPU:1, one launch (start us, length us, event | category | flops | bytes accessed | tf_op | source)
XLA Modules:
  0.0 43.3 jit_solution(8396457505504734439)
XLA Ops:
  0.6 0.0 copy-start
  0.6 26.1 %shard_map.162 = (bf16[128,3072]{1,0:T(8,128)(2,1)S(1)}, bf16[256,3072]{1,0:T(8,128)(2,1)S(1)}, bf16[256,2048]{1,0:T(8,128)(2,1)S(1)}, bf16[128,1536]{1,0:T(8,12...) custom-call(bf16[128,3072]{1,0:T(8,128)(2,1)} %bitcast.13, ...), custom_call_target="tpu_custom_call" | custom-call | tf_op jit(solution)/shard_map/pallas_call | solution.py:758
  26.8 0.0 copy-done
  26.8 0.0 copy-start.1
  26.8 0.0 copy-start.2
  26.8 2.0 %shard_map.164 = (bf16[136,1536]{1,0:T(8,128)(2,1)S(1)}, bf16[128,1536]{1,0:T(8,128)(2,1)S(1)}, f32[1,3072]{1,0:T(1,128)S(1)}) custom-call(bf16[256,2048]{1,0:T(8,128)(2,1)S(1)} %get-tuple-element.26.d_ref, bf16[256,3072]{1,0:T(8,128)(2,1)S(1)} %get-tuple-element.25.nm_ref, bf16[3072,2048]{1,0:T(8,128)(2,1)S(1)} %get-tuple-element.33.w_ref, ...), custom_call_target="tpu_custom_call" | custom-call | flops 1610612736 | bytes 6291456 | tf_op jit(solution)/shard_map/pallas_call | solution.py:822
  28.8 1.2 %collective-permute-start.1 = (bf16[136,1536]{1,0:T(8,128)(2,1)S(1)}, bf16[136,1536]{1,0:T(8,128)(2,1)S(1)}, u32[]{:S(2)}, u32[]{:S(2)}) collective-permute-start(bf16[136,1536]{1,0:T(8,128)(2,1)S(1)} %get-tuple-element.37), channel_id=1, source_target_pairs={{0,1},{1,0},{2,3},{3,2},{4,5},{5,4},{6,7},{7,6},{8,9},{9,8},{10,11... | collective-permute-start | bytes 1253384 | tf_op jit(solution)/shard_map/ppermute | solution.py:836
  30.0 0.3 collective-permute-start
  30.3 0.0 copy-done.1
  30.3 0.0 copy-done.2
  30.3 6.4 %shard_map.163 = (bf16[3072,1024]{1,0:T(8,128)(2,1)}, bf16[3072,512]{1,0:T(8,128)(2,1)}, bf16[3072,512]{1,0:T(8,128)(2,1)}, f32[64,3072]{1,0:T(8,128)}, f32[64,3072]{1,0:T(8,128)}) custom-call(bf16[256,3072]{1,0:T(8,128)(2,1)S(1)} %get-tuple-element.25.nm_ref, bf16[256,2048]{1,0:T(8,128)(2,1)S(1)} %get-tuple-element.26.d_ref, ...), custom_call_target="tpu_custom_call" | custom-call | flops 3221225472 | bytes 18874368 | tf_op jit(solution)/shard_map/pallas_call | solution.py:839
  36.7 5.1 %collective-permute-done.landed_a_ref = bf16[128,1536]{1,0:T(8,128)(2,1)S(1)} collective-permute-done((bf16[128,1536]{1,0:T(8,128)(2,1)S(1)}, bf16[128,1536]{1,0:T(8,128)(2,1)S(1)}, u32[]{:S(2)}, u32[]{:S(2)}) %collective-permute-start) | collective-permute-done | bytes 393248 | tf_op jit(solution)/shard_map/ppermute | solution.py:821
  41.8 0.0 collective-permute-done.1.landed_b_ref
  41.8 1.5 %shard_map.165 = (bf16[128,3072]{1,0:T(8,128)(2,1)}, f32[1,3072]{1,0:T(1,128)}) custom-call(bf16[128,3072]{1,0:T(8,128)(2,1)S(1)} %get-tuple-element.31.x_ref, bf16[128,1536]{1,0:T(8,128)(2,1)S(1)} %get-tuple-element.32.here_a_ref, bf16[128,1536]{1,0:T(8,128)(2,1)S(1)} %get-tuple-element.35.here_b_ref, f32[1,3072]{1,0:T(1,128)S(1)} %copy-done, ...), custom_call_target="tpu_custom_call" | custom-call | flops 4718592 | bytes 1572864 | tf_op jit(solution)/shard_map/pallas_call | solution.py:864
Async XLA Ops:
  0.6 26.1 %copy-start = (f32[1,3072]{1,0:T(1,128)S(1)}, f32[1,3072]{1,0:T(1,128)}, u32[]{:S(2)}) copy-start(f32[1,3072]{1,0:T(1,128)} %gain_ref.3) | copy-start | bytes 36868
  26.8 3.6 %copy-start.1 = (f32[64,3072]{1,0:T(8,128)S(1)}, f32[64,3072]{1,0:T(8,128)}, u32[]{:S(2)}) copy-start(f32[64,3072]{1,0:T(8,128)} %global_ref.1) | copy-start | bytes 2359300
  26.8 3.5 %copy-start.2 = (f32[64,3072]{1,0:T(8,128)S(1)}, f32[64,3072]{1,0:T(8,128)}, u32[]{:S(2)}) copy-start(f32[64,3072]{1,0:T(8,128)} %momentum_ref.1) | copy-start | bytes 2359300
  28.8 13.0 %collective-permute-start.1 = (bf16[136,1536]{1,0:T(8,128)(2,1)S(1)}, bf16[136,1536]{1,0:T(8,128)(2,1)S(1)}, u32[]{:S(2)}, u32[]{:S(2)}) collective-permute-start(bf16[136,1536]{1,0:T(8,128)(2,1)S(1)} %get-tuple-element.37), channel_id=1, source_target_pairs={{0,1},{1,0},{2,3},{3,2},{4,5},{5,4},{6,7},{7,6},{8,9},{9,8},{10,11... | collective-permute-start | bytes 1253384 | tf_op jit(solution)/shard_map/ppermute | solution.py:836
  30.0 11.7 %collective-permute-start = (bf16[128,1536]{1,0:T(8,128)(2,1)S(1)}, bf16[128,1536]{1,0:T(8,128)(2,1)S(1)}, u32[]{:S(2)}, u32[]{:S(2)}) collective-permute-start(bf16[128,1536]{1,0:T(8,128)(2,1)S(1)} %get-tuple-element.36), channel_id=1, source_target_pairs={{0,1},{1,0},{2,3},{3,2},{4,5},{5,4},{6,7},{7,6},{8,9},{9,8},{10,11... | collective-permute-start | bytes 1179656 | tf_op jit(solution)/shard_map/ppermute | solution.py:821
